TPU v7x, 32 devices: a whole 2x2x4 slice. The times are simulated.
32 devices in a mesh: lang: 2 (over y), clu: 16 (over z, x, core).
Axes of the slice: x: 2, y: 2, z: 4, core: 2. Of those that a mesh axis runs over, the one named last changes fastest.
Arguments:
- embeddings: bfloat16 [8192, 1024], P(('lang', 'clu')), parts along dimension 0, may hold values from -6 to 6
- assignment: int32 [8192, 1], P(('lang', 'clu')), parts along dimension 0, may hold values from 0 to 31; in each aligned block of 256 rows (0 to 255, 256 to 511, ...) at most 16 rows name the same one
Outputs:
- best_similarity: float32 [8192], P(('lang', 'clu')), parts along dimension 0
There are 2 independent parts, one for each index of `lang`. A program takes and returns all parts, laid end to end along the dimension named above; each array names one. Nothing has to cross between parts.
Inputs may be any that keep to these rules, and one draw needn't show every extreme that they name: `assignment`: in each aligned block of 256 rows (the rows of one device) no cluster is named by more than 16 rows; every cluster is named by some row.
All inputs are finite; a program needn't handle non-finite values.
Results may differ from a plain program's by a relative error of at most 0.0016.
Values may be sent and summed in bfloat16 or wider, within the bound.
No kernel may reach another device: no remote copies, remote signals or barrier semaphores. Data moves between devices by JAX's collectives and lax.ppermute only.
A program may use at most 64 MiB of HBM per device.

v0:
```python
import jax
import jax.numpy as jnp
from jax import lax
from jax.sharding import PartitionSpec as P

CLU_DEV = 2


EPS = 1e-06


def normalize(embeddings):
    values = embeddings.astype(jnp.float32)
    scale = lax.rsqrt(jnp.sum(values * values, axis=-1, keepdims=True) + EPS)
    return (values * scale).astype(jnp.bfloat16)


def slot_index(cluster, groups, most):
    count = cluster.shape[0]
    order = jnp.argsort(cluster, stable=True)
    ranked = cluster[order]
    first = jnp.searchsorted(ranked, ranked, side="left")
    rank_sorted = jnp.arange(count, dtype=jnp.int32) - first
    rank = jnp.zeros((count,), jnp.int32).at[order].set(rank_sorted)
    local = cluster % CLU_DEV
    owner = cluster // CLU_DEV
    return (local * groups + owner) * most + rank


def cluster_scores(pieces):
    rows, flags = pieces
    items = rows.shape[0]
    width = rows.shape[1] * rows.shape[2]
    rows = rows.reshape(items, width, rows.shape[3])
    flags = flags.reshape(items, width)
    offsets = jnp.arange(width, dtype=jnp.int32)
    distinct = offsets[:, None] != offsets[None, :]

    def single(pair):
        block, marks = pair
        gram = lax.dot_general(
            block, block, (((1,), (1,)), ((), ())), preferred_element_type=jnp.float32
        )
        keep = distinct & (marks > 0)[None, :]
        best = jnp.max(jnp.where(keep, gram, jnp.float32(-2.0)), axis=1)
        return jnp.maximum(best, jnp.float32(-1.0))

    best = lax.map(single, (rows, flags))
    return best.reshape(items, 1, width)


def shards(embeddings, assignment):
    groups = lax.axis_size("clu")
    count = embeddings.shape[0]
    width = embeddings.shape[1]
    most = 2 * count // (CLU_DEV * groups)
    unit = normalize(embeddings)
    cluster = assignment[:, 0]
    slot = slot_index(cluster, groups, most)
    total = CLU_DEV * groups * most
    outgoing = jnp.zeros((total, width), jnp.bfloat16).at[slot].set(unit)
    marks = jnp.zeros((total,), jnp.bfloat16).at[slot].set(jnp.ones((count,), jnp.bfloat16))
    outgoing = outgoing.reshape(CLU_DEV, groups, most, width)
    marks = marks.reshape(CLU_DEV, groups, most)
    arrived = (
        lax.all_to_all(outgoing, "clu", split_axis=1, concat_axis=2, tiled=True),
        lax.all_to_all(marks, "clu", split_axis=1, concat_axis=2, tiled=True),
    )
    best = cluster_scores(arrived)
    returned = lax.all_to_all(best, "clu", split_axis=2, concat_axis=1, tiled=True)
    return returned.reshape(total)[slot]


def solution(mesh):
    in_specs = (P(("lang", "clu"), None), P(("lang", "clu"), None))
    out_specs = P(("lang", "clu"))
    return jax.shard_map(shards, mesh=mesh, in_specs=in_specs, out_specs=out_specs, check_vma=False)
```

profile of v0, /device:TPU:0, one launch (start us, length us, event | category | flops | bytes accessed | tf_op | source)
XLA Modules:
  0.0 87.9 jit_solution(13854131566071930487)
XLA Ops:
  0.0 0.0 copy-start
  0.0 0.7 copy-done
  0.7 3.2 %sort.17 = (s32[256]{0:T(256)}, s32[256]{0:T(256)S(1)}) sort(s32[256]{0:T(256)S(1)} %bitcast.15, s32[256]{0:T(256)S(1)} %iota.14), dimensions={0}, to_apply=%region_0.0 | sort | flops 2048 | bytes 4096 | tf_op jit(solution)/shard_map/jit(argsort)/sort | solution.py:20
  3.9 1.9 %gather_fusion.1 = s32[256]{0:T(256)S(1)} fusion(s32[256]{0:T(256)S(1)} %bitcast.16, s32[1024]{0:T(1024)S(1)} %pad_clamp_fusion.2), kind=kCustom, calls=%fused_computation.1 | custom fusion | bytes 3072 | tf_op jit(solution)/shard_map/gather | solution.py:21
  5.8 0.0 copy-start.1
  5.8 18.4 %while.37 = (s32[]{:T(128)}, u32[256]{0:T(256)S(1)}, u32[256]{0:T(256)S(1)}, s32[256]{0:T(256)S(1)}, s32[]{:T(128)}, /*index=5*/s32[]{:T(128)}, s32[]{}) while((s32[]{:T(128)}, u32[256]{0:T(256)S(1)}, u32[256]{0:T(256)S(1)}, s32[256]{0:T(256)S(1)}, s32[]{:T(128)}, /*index=5*/s32[]{:T(128)}, s32[]{}) %tuple.52), condition=%wide.region_2.3_spmd.clone, body=%wide.region_1.0_spmd.clone.sunk | while | flops 5636 | bytes 22117 | solution.py:22
  5.9 1.9 %gather_fusion = s32[256]{0:T(256)S(1)} fusion(s32[256]{0:T(256)S(1)} %get-tuple-element.217, u32[1024]{0:T(1024)S(1)} %pad_clamp_fusion.4), kind=kCustom, calls=%fused_computation.clone.clone.1 | custom fusion | bytes 3072 | tf_op jit(solution)/shard_map/jit(searchsorted)/jit(_searchsorted_scan_impl)/vmap(jit(_searchsorted_scan_impl))/while/body/eval_jaxpr/gather | solution.py:22
  7.9 1.9 %gather_fusion = s32[256]{0:T(256)S(1)} fusion(s32[256]{0:T(256)S(1)} %get-tuple-element.217, u32[1024]{0:T(1024)S(1)} %pad_clamp_fusion.4), kind=kCustom, calls=%fused_computation.clone.clone.1 | custom fusion | bytes 3072 | tf_op jit(solution)/shard_map/jit(searchsorted)/jit(_searchsorted_scan_impl)/vmap(jit(_searchsorted_scan_impl))/while/body/eval_jaxpr/gather | solution.py:22
  9.9 1.9 %gather_fusion = s32[256]{0:T(256)S(1)} fusion(s32[256]{0:T(256)S(1)} %get-tuple-element.217, u32[1024]{0:T(1024)S(1)} %pad_clamp_fusion.4), kind=kCustom, calls=%fused_computation.clone.clone.1 | custom fusion | bytes 3072 | tf_op jit(solution)/shard_map/jit(searchsorted)/jit(_searchsorted_scan_impl)/vmap(jit(_searchsorted_scan_impl))/while/body/eval_jaxpr/gather | solution.py:22
  12.0 1.9 %gather_fusion = s32[256]{0:T(256)S(1)} fusion(s32[256]{0:T(256)S(1)} %get-tuple-element.217, u32[1024]{0:T(1024)S(1)} %pad_clamp_fusion.4), kind=kCustom, calls=%fused_computation.clone.clone.1 | custom fusion | bytes 3072 | tf_op jit(solution)/shard_map/jit(searchsorted)/jit(_searchsorted_scan_impl)/vmap(jit(_searchsorted_scan_impl))/while/body/eval_jaxpr/gather | solution.py:22
  14.0 1.9 %gather_fusion = s32[256]{0:T(256)S(1)} fusion(s32[256]{0:T(256)S(1)} %get-tuple-element.217, u32[1024]{0:T(1024)S(1)} %pad_clamp_fusion.4), kind=kCustom, calls=%fused_computation.clone.clone.1 | custom fusion | bytes 3072 | tf_op jit(solution)/shard_map/jit(searchsorted)/jit(_searchsorted_scan_impl)/vmap(jit(_searchsorted_scan_impl))/while/body/eval_jaxpr/gather | solution.py:22
  16.1 1.9 %gather_fusion = s32[256]{0:T(256)S(1)} fusion(s32[256]{0:T(256)S(1)} %get-tuple-element.217, u32[1024]{0:T(1024)S(1)} %pad_clamp_fusion.4), kind=kCustom, calls=%fused_computation.clone.clone.1 | custom fusion | bytes 3072 | tf_op jit(solution)/shard_map/jit(searchsorted)/jit(_searchsorted_scan_impl)/vmap(jit(_searchsorted_scan_impl))/while/body/eval_jaxpr/gather | solution.py:22
  18.1 1.9 %gather_fusion = s32[256]{0:T(256)S(1)} fusion(s32[256]{0:T(256)S(1)} %get-tuple-element.217, u32[1024]{0:T(1024)S(1)} %pad_clamp_fusion.4), kind=kCustom, calls=%fused_computation.clone.clone.1 | custom fusion | bytes 3072 | tf_op jit(solution)/shard_map/jit(searchsorted)/jit(_searchsorted_scan_impl)/vmap(jit(_searchsorted_scan_impl))/while/body/eval_jaxpr/gather | solution.py:22
  20.1 1.9 %gather_fusion = s32[256]{0:T(256)S(1)} fusion(s32[256]{0:T(256)S(1)} %get-tuple-element.217, u32[1024]{0:T(1024)S(1)} %pad_clamp_fusion.4), kind=kCustom, calls=%fused_computation.clone.clone.1 | custom fusion | bytes 3072 | tf_op jit(solution)/shard_map/jit(searchsorted)/jit(_searchsorted_scan_impl)/vmap(jit(_searchsorted_scan_impl))/while/body/eval_jaxpr/gather | solution.py:22
  22.2 1.9 %gather_fusion = s32[256]{0:T(256)S(1)} fusion(s32[256]{0:T(256)S(1)} %get-tuple-element.217, u32[1024]{0:T(1024)S(1)} %pad_clamp_fusion.4), kind=kCustom, calls=%fused_computation.clone.clone.1 | custom fusion | bytes 3072 | tf_op jit(solution)/shard_map/jit(searchsorted)/jit(_searchsorted_scan_impl)/vmap(jit(_searchsorted_scan_impl))/while/body/eval_jaxpr/gather | solution.py:22
  24.2 1.4 %scatter_custom_fusion = s32[256]{0:T(256)S(1)} fusion(s32[256]{0:T(256)S(1)} %compare_select_fusion.1, s32[256]{0:T(256)S(1)} %convert_subtract_fusion, s32[]{:T(128)} %constant.83.clone.1), kind=kCustom, calls=%fused_computation.42 | custom fusion | bytes 1028 | tf_op jit(solution)/shard_map/scatter | solution.py:24
  25.6 2.2 %scatter_custom_fusion.1 = bf16[512]{0:T(512)(128)(2,1)S(1)} fusion(s32[256]{0:T(256)S(1)} %compare_select_fusion, bf16[256]{0:T(256)(128)(2,1)S(1)} %broadcast.47, bf16[]{:T(256)} %constant.85.clone.1), kind=kCustom, calls=%fused_computation.44 | custom fusion | bytes 1026 | tf_op jit(solution)/shard_map/scatter | solution.py:62
  27.8 0.1 reshape.45
  27.9 0.6 copy.5
  28.5 7.4 %all-to-all-start = ((bf16[2,16,16]{2,0,1:T(2,128)(2,1)}), bf16[2,16,16]{2,0,1:T(2,128)(2,1)S(1)}, u32[]{:S(2)}, u32[]{:S(2)}) async-start(bf16[2,16,16]{2,0,1:T(2,128)(2,1)} %copy.5), calls=%async_computation | async-start | bytes 16384 | tf_op jit(solution)/shard_map/all_to_all | solution.py:67
  35.9 0.0 copy-done.1
  35.9 0.2 fusion.9
  36.1 2.0 %scatter_custom_fusion.2 = bf16[512,1024]{1,0:T(8,128)(2,1)S(1)} fusion(s32[256]{0:T(256)S(1)} %compare_select_fusion, bf16[256,1024]{1,0:T(8,128)(2,1)S(1)} %copy-done.1, f32[256]{0:T(256)S(1)} %add_rsqrt_fusion, bf16[]{:T(256)} %constant.85.clone.1), kind=kCustom, calls=%fused_computation.26 | custom fusion | flops 786432 | bytes 1573890 | tf_op jit(solution)/shard_map/scatter | solution.py:61
  38.1 1.1 %copy.7 = bf16[2,16,16,1024]{3,2,0,1:T(8,128)(2,1)} copy(bf16[2,16,16,1024]{3,2,1,0:T(8,128)(2,1)S(1)} %bitcast.19) | data formatting | bytes 2097152 | tf_op jit(solution)/shard_map/reshape | solution.py:63
  39.2 3.2 %all-to-all-done = bf16[2,16,16]{2,0,1:T(2,128)(2,1)S(1)} async-done(((bf16[2,16,16]{2,0,1:T(2,128)(2,1)}), bf16[2,16,16]{2,0,1:T(2,128)(2,1)S(1)}, u32[]{:S(2)}, u32[]{:S(2)}) %all-to-all-start) | async-done | bytes 1056 | tf_op jit(solution)/shard_map/all_to_all | solution.py:67
  42.3 3.7 %all-to-all-start.1 = ((bf16[2,16,16,1024]{3,2,0,1:T(8,128)(2,1)}), bf16[2,16,16,1024]{3,2,0,1:T(8,128)(2,1)S(1)}, u32[]{:S(2)}, u32[]{:S(2)}) async-start(bf16[2,16,16,1024]{3,2,0,1:T(8,128)(2,1)} %copy.7), calls=%async_computation.1 | async-start | bytes 2097152 | tf_op jit(solution)/shard_map/all_to_all | solution.py:66
  46.0 0.1 reshape.46
  46.1 22.7 %all-to-all-done.1 = bf16[2,16,16,1024]{3,2,0,1:T(8,128)(2,1)S(1)} async-done(((bf16[2,16,16,1024]{3,2,0,1:T(8,128)(2,1)}), bf16[2,16,16,1024]{3,2,0,1:T(8,128)(2,1)S(1)}, u32[]{:S(2)}, u32[]{:S(2)}) %all-to-all-start.1) | async-done | bytes 1048608 | tf_op jit(solution)/shard_map/all_to_all | solution.py:66
  68.8 0.1 copy.8
  68.9 0.9 %while.36 = (s32[]{:T(128)}, f32[2,256]{1,0:T(2,128)S(1)}, bf16[2,256]{1,0:T(2,128)(2,1)S(1)}, bf16[2,256,1024]{2,1,0:T(8,128)(2,1)S(1)}, s32[]{:T(128)}, /*index=5*/s32[]{:T(128)}) while((s32[]{:T(128)}, f32[2,256]{1,0:T(2,128)S(1)}, bf16[2,256]{1,0:T(2,128)(2,1)S(1)}, bf16[2,256,1024]{2,1,0:T(8,128)(2,1)S(1)}, s32[]{:T(128)}, ...), condition=%wide.region_9.10_spmd.clone, body=%wide.region_7.9_spmd.clone.sunk | while | flops 134480640 | bytes 530769 | solution.py:48
  69.0 0.4 fusion.26
  69.4 0.4 fusion.26
  69.8 0.8 copy.9
  70.6 6.7 %all-to-all-start.2 = ((f32[2,1,256]{0,1,2:T(1,128)}), f32[2,1,256]{0,1,2:T(1,128)S(1)}, u32[]{:S(2)}, u32[]{:S(2)}) async-start(f32[2,1,256]{0,1,2:T(1,128)} %bitcast.3), calls=%async_computation.2 | async-start | bytes 262144 | tf_op jit(solution)/shard_map/all_to_all | solution.py:70
  77.4 7.9 %all-to-all-done.2 = f32[2,1,256]{0,1,2:T(1,128)S(1)} async-done(((f32[2,1,256]{0,1,2:T(1,128)}), f32[2,1,256]{0,1,2:T(1,128)S(1)}, u32[]{:S(2)}, u32[]{:S(2)}) %all-to-all-start.2) | async-done | bytes 2080 | tf_op jit(solution)/shard_map/all_to_all | solution.py:70
  85.3 0.1 copy.10
  85.4 2.5 %gather_fusion.2 = f32[256]{0:T(256)} fusion(f32[512]{0:T(512)S(1)} %bitcast.18, s32[1024]{0:T(1024)S(1)} %pad_clamp_fusion.1), kind=kCustom, calls=%fused_computation.2 | custom fusion | bytes 3072 | tf_op jit(solution)/shard_map/gather | solution.py:71
  (64 shorter events, 0.6 us)
Async XLA Ops:
  0.0 0.7 copy-start
  5.8 30.1 %copy-start.1 = (bf16[256,1024]{1,0:T(8,128)(2,1)S(1)}, bf16[256,1024]{1,0:T(8,128)(2,1)}, u32[]{:S(2)}) copy-start(bf16[256,1024]{1,0:T(8,128)(2,1)} %param.6) | copy-start | bytes 1572868
  28.5 13.8 %all-to-all-start = ((bf16[2,16,16]{2,0,1:T(2,128)(2,1)}), bf16[2,16,16]{2,0,1:T(2,128)(2,1)S(1)}, u32[]{:S(2)}, u32[]{:S(2)}) async-start(bf16[2,16,16]{2,0,1:T(2,128)(2,1)} %copy.5), calls=%async_computation | async-start | bytes 16384 | tf_op jit(solution)/shard_map/all_to_all | solution.py:67
  42.3 26.5 %all-to-all-start.1 = ((bf16[2,16,16,1024]{3,2,0,1:T(8,128)(2,1)}), bf16[2,16,16,1024]{3,2,0,1:T(8,128)(2,1)S(1)}, u32[]{:S(2)}, u32[]{:S(2)}) async-start(bf16[2,16,16,1024]{3,2,0,1:T(8,128)(2,1)} %copy.7), calls=%async_computation.1 | async-start | bytes 2097152 | tf_op jit(solution)/shard_map/all_to_all | solution.py:66
  70.6 14.6 %all-to-all-start.2 = ((f32[2,1,256]{0,1,2:T(1,128)}), f32[2,1,256]{0,1,2:T(1,128)S(1)}, u32[]{:S(2)}, u32[]{:S(2)}) async-start(f32[2,1,256]{0,1,2:T(1,128)} %bitcast.3), calls=%async_computation.2 | async-start | bytes 262144 | tf_op jit(solution)/shard_map/all_to_all | solution.py:70
where the time goes:
time: 88.2 us; the launch traced here: 87.9 us
  waiting for transfers between devices  33.8 us (38%)
  local copies, waits for them, and re-layouts  29.1 us (33%)
  starting transfers between devices  17.8 us (20%)
  other arithmetic  5.78 us (7%)
    all_to_all x1, waiting for transfers between devices, shards(): lax.all_to_all(outgoing, 'clu', split_axis=1, concat_axis=2, tiled=True)  22.7 us
    gather x9, local copies, waits for them, and re-layouts, slot_index(): first = jnp.searchsorted(ranked, ranked, side='left')  17.5 us
    all_to_all x1, waiting for transfers between devices, shards(): lax.all_to_all(best, 'clu', split_axis=2, concat_axis=1, tiled=True)  7.89 us
    all_to_all x1, starting transfers between devices, shards(): lax.all_to_all(marks, 'clu', split_axis=1, concat_axis=2, tiled=True)  7.39 us
    all_to_all x1, starting transfers between devices, shards(): lax.all_to_all(best, 'clu', split_axis=2, concat_axis=1, tiled=True)  6.74 us
    all_to_all x1, starting transfers between devices, shards(): lax.all_to_all(outgoing, 'clu', split_axis=1, concat_axis=2, tiled=True)  3.65 us
    all_to_all x1, waiting for transfers between devices, shards(): lax.all_to_all(marks, 'clu', split_axis=1, concat_axis=2, tiled=True)  3.18 us
    sort x1, other arithmetic, slot_index(): order = jnp.argsort(cluster, stable=True)  3.16 us
  transfers between devices with their start and end apart: 3, of which 3 were waited for; matrix products, arithmetic and copies ran while one was open for 4% of the time, Pallas kernels for 0%

commit v1 on v0

v1 whole, which is shorter than its diff:
```python
import functools

import jax
import jax.numpy as jnp
from jax import lax
from jax.experimental import pallas as pl
from jax.experimental.pallas import tpu as pltpu
from jax.sharding import PartitionSpec as P

CLU_DEV = 2
EPS = 1e-06
PAD = 2.0
LANES = 128


def pack_kernel(most, rows_ref, cluster_ref, out_ref, slot_ref):
    count = rows_ref.shape[0]
    slots = out_ref.shape[0]
    labels = slots // most
    cluster = cluster_ref[...]
    member = lax.broadcasted_iota(jnp.int32, (labels, count), 0) == cluster
    onehot = member.astype(jnp.bfloat16)
    before = (
        lax.broadcasted_iota(jnp.int32, (count, count), 0)
        < lax.broadcasted_iota(jnp.int32, (count, count), 1)
    ).astype(jnp.bfloat16)
    prior = jnp.dot(onehot, before, preferred_element_type=jnp.float32)
    rank = jnp.sum(jnp.where(member, prior, 0.0), axis=0, keepdims=True)
    slot = cluster * most + rank.astype(jnp.int32)
    slot_ref[...] = slot
    place = (lax.broadcasted_iota(jnp.int32, (slots, count), 0) == slot).astype(jnp.bfloat16)
    values = rows_ref[...].astype(jnp.float32)
    scale = lax.rsqrt(jnp.sum(values * values, axis=-1, keepdims=True) + EPS)
    unit = (values * scale).astype(jnp.bfloat16)
    packed = jnp.dot(place, unit, preferred_element_type=jnp.float32)
    live = jnp.sum(place.astype(jnp.float32), axis=1, keepdims=True) > 0
    first = lax.broadcasted_iota(jnp.int32, packed.shape, 1) == 0
    out_ref[...] = jnp.where(first & ~live, PAD, packed).astype(jnp.bfloat16)


def score_kernel(most, rows_ref, out_ref):
    slots = rows_ref.shape[0]
    groups = out_ref.shape[0]
    rows = rows_ref[...]
    gram = lax.dot_general(
        rows, rows, (((1,), (1,)), ((), ())), preferred_element_type=jnp.float32
    )
    live = rows[:, :1].astype(jnp.float32) < 1.5
    i = lax.broadcasted_iota(jnp.int32, (slots, slots), 0)
    j = lax.broadcasted_iota(jnp.int32, (slots, slots), 1)
    keep = live & (i != j) & (((i // most) ^ (j // most)) % CLU_DEV == 0)
    best = jnp.max(jnp.where(keep, gram, -1.0), axis=0, keepdims=True)
    share = LANES * groups // slots
    for p in range(groups):
        out_ref[p] = best[:, p // share * LANES : (p // share + 1) * LANES]


def pick_kernel(best_ref, slot_ref, out_ref):
    groups = best_ref.shape[0]
    count = slot_ref.shape[1]
    width = 2 * count // groups
    slot = slot_ref[...]
    lane = lax.axis_index("clu") % (LANES // width) * width + slot % width
    inner = (lax.broadcasted_iota(jnp.int32, (LANES, count), 0) == lane).astype(jnp.float32)
    table = jnp.dot(
        best_ref[:, 0, :], inner, precision=lax.Precision.HIGHEST,
        preferred_element_type=jnp.float32,
    )
    outer = lax.broadcasted_iota(jnp.int32, (groups, count), 0) == slot // width
    out_ref[...] = jnp.sum(jnp.where(outer, table, 0.0), axis=0, keepdims=True)


def shards(embeddings, assignment):
    groups = lax.axis_size("clu")
    count, width = embeddings.shape
    most = 2 * count // (CLU_DEV * groups)
    slots = CLU_DEV * groups * most
    vmem = pl.BlockSpec(memory_space=pltpu.VMEM)
    packed, slot = pl.pallas_call(
        functools.partial(pack_kernel, most),
        out_shape=(
            jax.ShapeDtypeStruct((slots, width), jnp.bfloat16),
            jax.ShapeDtypeStruct((1, count), jnp.int32),
        ),
        in_specs=[vmem, vmem],
        out_specs=(vmem, vmem),
        name="pack",
    )(embeddings, assignment.reshape(1, count))
    packed = packed.reshape(groups, CLU_DEV * most, width)
    arrived = lax.all_to_all(packed, "clu", split_axis=0, concat_axis=0, tiled=True)
    best = pl.pallas_call(
        functools.partial(score_kernel, most),
        out_shape=jax.ShapeDtypeStruct((groups, 1, LANES), jnp.float32),
        in_specs=[vmem],
        out_specs=vmem,
        name="score",
    )(arrived.reshape(slots, width))
    returned = lax.all_to_all(best, "clu", split_axis=0, concat_axis=0, tiled=True)
    out = pl.pallas_call(
        pick_kernel,
        out_shape=jax.ShapeDtypeStruct((1, count), jnp.float32),
        in_specs=[vmem, vmem],
        out_specs=vmem,
        name="pick",
    )(returned, slot)
    return out.reshape(count)


def solution(mesh):
    in_specs = (P(("lang", "clu"), None), P(("lang", "clu"), None))
    out_specs = P(("lang", "clu"))
    return jax.shard_map(shards, mesh=mesh, in_specs=in_specs, out_specs=out_specs, check_vma=False)
```

time: 88.2 us -> 50.9 us (0.58)
  blocking collectives: 0 us -> 43.6 us
  waiting for transfers between devices: 33.8 us -> 0 us
  local copies, waits for them, and re-layouts: 29.1 us -> 0 us
  starting transfers between devices: 17.8 us -> 0 us
  Pallas kernels: 0 us -> 7.01 us
  other arithmetic: 5.78 us -> 0 us
    all_to_all x0 -> x2, blocking collectives: none -> 43.6 us  [the longest x1 32.2 us: shards(): lax.all_to_all(packed, 'clu', split_axis=0, concat_axis=0, tiled=True)]
    all_to_all x3 -> x0, waiting for transfers between devices: 33.8 us -> none  [the longest x1 22.7 us: shards(): lax.all_to_all(outgoing, 'clu', split_axis=1, concat_axis=2, tiled=True)]
    gather x11 -> x0, local copies, waits for them, and re-layouts: 22 us -> none  [the longest x9 17.5 us: slot_index(): first = jnp.searchsorted(ranked, ranked, side='left')]
    all_to_all x3 -> x0, starting transfers between devices: 17.8 us -> none  [the longest x1 7.39 us: shards(): lax.all_to_all(marks, 'clu', split_axis=1, concat_axis=2, tiled=True)]
    pallas_call x0 -> x3, Pallas kernels: none -> 7.01 us  [the longest x1 2.83 us: shards(): pl.pallas_call(functools.partial(score_kernel, most), out_shape=jax.Shape...]
    scatter x2 -> x0, local copies, waits for them, and re-layouts: 3.56 us -> none  [the longest x1 2.16 us: shards(): jnp.zeros((total,), jnp.bfloat16).at[slot]]
    sort x1 -> x0, other arithmetic: 3.16 us -> none  [slot_index(): order = jnp.argsort(cluster, stable=True)]
    scatter x1 -> x0, other arithmetic: 1.98 us -> none  [shards(): outgoing = jnp.zeros((total, width), jnp.bfloat16).at[slot].set(unit)]
  transfers between devices with their start and end apart: 3 -> 0, of which waited for: 3 -> 0; matrix products, arithmetic and copies ran while one was open for 4% -> 0% of each run, Pallas kernels for 0% -> 0%
where the time goes in v1:
time: 50.9 us; the launch traced here: 50.6 us
  blocking collectives  43.6 us (86%)
  Pallas kernels  7.01 us (14%)
    all_to_all x1, blocking collectives, shards(): lax.all_to_all(packed, 'clu', split_axis=0, concat_axis=0, tiled=True)  32.2 us
    all_to_all x1, blocking collectives, shards(): lax.all_to_all(best, 'clu', split_axis=0, concat_axis=0, tiled=True)  11.4 us
    pallas_call x1, Pallas kernels, shards(): pl.pallas_call(functools.partial(score_kernel, most), out_shape=jax.Shape...  2.83 us
    pallas_call x1, Pallas kernels, shards(): pl.pallas_call(functools.partial(pack_kernel, most), out_shape=(jax.Shape...  2.72 us
    pallas_call x1, Pallas kernels, shards(): pl.pallas_call(pick_kernel, out_shape=jax.ShapeDtypeStruct((1, count), jn...  1.46 us

profile of v1, /device:TPU:0, one launch (start us, length us, event | category | flops | bytes accessed | tf_op | source)
XLA Modules:
  0.0 50.6 jit_solution(6638028271233176982)
XLA Ops:
  0.0 2.7 %pack.1 = (bf16[512,1024]{1,0:T(8,128)(2,1)}, s32[1,256]{1,0:T(1,128)}) custom-call(bf16[256,1024]{1,0:T(8,128)(2,1)} %rows_ref.1, s32[1,256]{1,0:T(1,128)} %bitcast.6), custom_call_target="tpu_custom_call" | custom-call | tf_op jit(solution)/shard_map/pack/pallas_call | solution.py:79
  2.7 32.2 %all_to_all.10 = bf16[16,32,1024]{2,1,0:T(8,128)(2,1)} all-to-all(bf16[16,32,1024]{2,1,0:T(8,128)(2,1)} %bitcast.5), channel_id=1, replica_groups=mesh['lang'=2,'clu'=16] {'clu'}, dimensions={0} | all-to-all | bytes 2097152 | tf_op jit(solution)/shard_map/all_to_all | solution.py:90
  34.9 2.8 %score.1 = f32[16,1,128]{2,1,0:T(1,128)} custom-call(bf16[512,1024]{1,0:T(8,128)(2,1)} %bitcast.4), custom_call_target="tpu_custom_call" | custom-call | tf_op jit(solution)/shard_map/score/pallas_call | solution.py:91
  37.7 11.4 %all_to_all.11.best_ref = f32[16,1,128]{2,1,0:T(1,128)} all-to-all(f32[16,1,128]{2,1,0:T(1,128)} %score.1), channel_id=1, replica_groups=mesh['lang'=2,'clu'=16] {'clu'}, dimensions={0} | all-to-all | bytes 16384 | tf_op jit(solution)/shard_map/all_to_all | solution.py:98
  49.1 1.5 %pick.1 = f32[1,256]{1,0:T(1,128)} custom-call(f32[16,1,128]{2,1,0:T(1,128)} %all_to_all.11.best_ref, s32[1,256]{1,0:T(1,128)} %get-tuple-element.8.slot_ref), custom_call_target="tpu_custom_call" | custom-call | tf_op jit(solution)/shard_map/pick/pallas_call | solution.py:99

commit v2 on v1

v2 whole, which is shorter than its diff:
```python
import functools

import jax
import jax.numpy as jnp
from jax import lax
from jax.experimental import pallas as pl
from jax.experimental.pallas import tpu as pltpu
from jax.sharding import PartitionSpec as P


CLU_DEV = 2
EPS = 1e-06
PAD = 2.0
LANES = 128
GRANT = 8 * 1024 * 1024
VMEM = pl.BlockSpec(memory_space=pltpu.VMEM)
HBM = pl.BlockSpec(memory_space=pltpu.HBM)


def call(kernel, out_shape, args, in_specs=None, scratch=(), flops=1 << 24, grant=GRANT):
    return pl.pallas_call(
        kernel,
        out_shape=out_shape,
        in_specs=in_specs or [VMEM] * len(args),
        out_specs=jax.tree.map(lambda _: VMEM, out_shape),
        scratch_shapes=scratch,
        compiler_params=pltpu.CompilerParams(vmem_limit_bytes=grant),
        cost_estimate=pl.CostEstimate(flops=flops, bytes_accessed=1 << 20, transcendentals=0),
    )(*args)


def block_order(k):
    return k ^ jnp.where(k >= 2, 1, 0)


def rank_of(cluster, labels):
    count = cluster.shape[1]
    member = lax.broadcasted_iota(jnp.int32, (labels, count), 0) == cluster
    before = (
        lax.broadcasted_iota(jnp.int32, (count, count), 0)
        < lax.broadcasted_iota(jnp.int32, (count, count), 1)
    ).astype(jnp.bfloat16)
    prior = jnp.dot(member.astype(jnp.bfloat16), before, preferred_element_type=jnp.float32)
    return jnp.sum(jnp.where(member, prior, 0.0), axis=0, keepdims=True).astype(jnp.int32)


def pack_kernel(sizes, most, labels, relative, rows_hbm, cluster_hbm, *refs):
    *out_refs, rank_ref, cluster_ref, rows_ref, cluster_vmem, sems = refs
    load_cluster = pltpu.make_async_copy(cluster_hbm, cluster_vmem, sems.at[0])
    load_rows = pltpu.make_async_copy(rows_hbm, rows_ref, sems.at[1])
    load_cluster.start()
    load_rows.start()
    load_cluster.wait()
    cluster = cluster_vmem[...]
    rank = rank_of(cluster, labels)
    rank_ref[...] = rank
    cluster_ref[...] = cluster
    owner = cluster // CLU_DEV
    if relative:
        owner = block_order(owner ^ lax.axis_index("clu"))
    position = (owner * CLU_DEV + cluster % CLU_DEV) * most + rank
    slots = sum(sizes)
    count = rows_ref.shape[0]
    place = lax.broadcasted_iota(jnp.int32, (slots, count), 0) == position
    live = jnp.sum(place.astype(jnp.float32), axis=1, keepdims=True) > 0
    load_rows.wait()
    values = rows_ref[...].astype(jnp.float32)
    scale = lax.rsqrt(jnp.sum(values * values, axis=-1, keepdims=True) + EPS)
    unit = (values * scale).astype(jnp.bfloat16)
    packed = jnp.dot(place.astype(jnp.bfloat16), unit, preferred_element_type=jnp.float32)
    first = lax.broadcasted_iota(jnp.int32, (slots, LANES), 1) == 0
    head = jnp.where(first & ~live, PAD, packed[:, :LANES]).astype(jnp.bfloat16)
    rest = packed[:, LANES:].astype(jnp.bfloat16)
    start = 0
    for size, out_ref in zip(sizes, out_refs):
        out_ref[:, :LANES] = head[start:start + size]
        out_ref[:, LANES:] = rest[start:start + size]
        start += size


def best_of(rows, keep=None):
    slots = rows.shape[0]
    gram = lax.dot_general(
        rows, rows, (((1,), (1,)), ((), ())), preferred_element_type=jnp.float32
    )
    live = rows[:, :1].astype(jnp.float32) < 1.5
    i = lax.broadcasted_iota(jnp.int32, (slots, slots), 0)
    j = lax.broadcasted_iota(jnp.int32, (slots, slots), 1)
    mask = live & (i != j)
    if keep is not None:
        mask &= keep(i, j)
    return jnp.max(jnp.where(mask, gram, -1.0), axis=0, keepdims=True)


def score_blocks_kernel(most, where, *refs):
    *row_refs, out_ref = refs
    me = lax.axis_index("clu")
    for local in range(CLU_DEV):
        rows = jnp.concatenate(
            [row_refs[n][start + local * most:start + (local + 1) * most] for n, start in where],
            axis=0,
        )
        best = best_of(rows)
        for k in range(len(where)):
            lane = k * most // LANES * LANES
            out_ref[me ^ k, pl.ds(local, 1), :] = best[:, lane:lane + LANES]


def score_all_kernel(most, rows_ref, out_ref):
    groups = out_ref.shape[0]
    best = best_of(rows_ref[...], lambda i, j: ((i // most) ^ (j // most)) % CLU_DEV == 0)
    share = LANES // (CLU_DEV * most)
    for p in range(groups):
        out_ref[p] = best[:, p // share * LANES:(p // share + 1) * LANES]


def pick_kernel(most, relative, best_ref, rank_ref, cluster_ref, out_ref):
    groups, lines = best_ref.shape[:2]
    count = rank_ref.shape[1]
    me = lax.axis_index("clu")
    cluster = cluster_ref[...]
    owner = cluster // CLU_DEV
    local = cluster % CLU_DEV
    if relative:
        lane = (owner ^ me) * most + rank_ref[...]
    else:
        lane = (me * CLU_DEV + local) * most + rank_ref[...]
    inner = (lax.broadcasted_iota(jnp.int32, (LANES, count), 0) == lane % LANES).astype(jnp.float32)
    total = jnp.zeros((1, count), jnp.float32)
    for line in range(lines):
        table = jnp.dot(
            best_ref[:, line, :], inner, precision=lax.Precision.HIGHEST,
            preferred_element_type=jnp.float32,
        )
        outer = lax.broadcasted_iota(jnp.int32, (groups, count), 0) == owner
        if lines > 1:
            outer &= local == line
        total += jnp.sum(jnp.where(outer, table, 0.0), axis=0, keepdims=True)
    out_ref[...] = total


def pack(embeddings, assignment, sizes, most, labels, relative):
    count, width = embeddings.shape
    line = jax.ShapeDtypeStruct((1, count), jnp.int32)
    out = tuple(jax.ShapeDtypeStruct((size, width), jnp.bfloat16) for size in sizes)
    *packed, rank, cluster = call(
        functools.partial(pack_kernel, sizes, most, labels, relative),
        (*out, line, line),
        (
            pltpu.with_memory_space_constraint(embeddings, pltpu.HBM),
            pltpu.with_memory_space_constraint(assignment.reshape(1, count), pltpu.HBM),
        ),
        in_specs=[HBM, HBM],
        scratch=[
            pltpu.VMEM((count, width), jnp.bfloat16),
            pltpu.VMEM((1, count), jnp.int32),
            pltpu.SemaphoreType.DMA((2,)),
        ],
    )
    return packed, rank, cluster


def swap(array, k):
    groups = lax.axis_size("clu")
    return lax.ppermute(array, "clu", [(i, i ^ k) for i in range(groups)])


def exchange_blocks(embeddings, assignment, most, labels):
    groups = lax.axis_size("clu")
    block = CLU_DEV * most
    chips = groups // 2
    last = chips // 2
    sizes = [block, block]
    for m in range(1, chips):
        sizes += [block, block] if m == last else [2 * block]
    packed, rank, cluster = pack(embeddings, assignment, tuple(sizes), most, labels, True)
    own, partner, *others = packed
    sent = {}
    for m in range(1, chips):
        sent[m] = [others.pop(0) for _ in range(2 if m == last else 1)]
    arrived = {}
    for m in range(1, chips):
        arrived[m] = []
        for n, array in enumerate(sent[m]):
            arrived[m].append(swap(array, 2 * m + 1 - n))
    args = [own, swap(partner, 1)]
    where = [(0, 0), (1, 0)]
    for m in range(1, chips):
        if m == last:
            far, near = arrived[m]
            args += [near, far]
            where += [(len(args) - 2, 0), (len(args) - 1, 0)]
        else:
            both = arrived[m][0]
            args += [swap(both[block:], 1), both]
            where += [(len(args) - 2, 0), (len(args) - 1, 0)]
    best = call(
        functools.partial(score_blocks_kernel, most, tuple(where)),
        jax.ShapeDtypeStruct((groups, CLU_DEV, LANES), jnp.float32), args,
    )
    return best, rank, cluster


def exchange_all(embeddings, assignment, most, labels):
    groups = lax.axis_size("clu")
    width = embeddings.shape[1]
    slots = labels * most
    (packed,), rank, cluster = pack(embeddings, assignment, (slots,), most, labels, False)
    arrived = lax.all_to_all(
        packed.reshape(groups, slots // groups, width), "clu",
        split_axis=0, concat_axis=0, tiled=True,
    )
    best = call(
        functools.partial(score_all_kernel, most),
        jax.ShapeDtypeStruct((groups, 1, LANES), jnp.float32), (arrived.reshape(slots, width),),
    )
    return best, rank, cluster


def uses_blocks(groups, most):
    return most % 16 == 0 and groups >= 4 and groups & (groups - 1) == 0


def shards(embeddings, assignment):
    groups = lax.axis_size("clu")
    count = embeddings.shape[0]
    most = 2 * count // (CLU_DEV * groups)
    labels = CLU_DEV * groups
    relative = uses_blocks(groups, most)
    exchange = exchange_blocks if relative else exchange_all
    best, rank, cluster = exchange(embeddings, assignment, most, labels)
    returned = lax.all_to_all(best, "clu", split_axis=0, concat_axis=0, tiled=True)
    out = call(
        functools.partial(pick_kernel, most, relative),
        jax.ShapeDtypeStruct((1, count), jnp.float32), (returned, rank, cluster),
    )
    return out.reshape(count)


def solution(mesh):
    in_specs = (P(("lang", "clu"), None), P(("lang", "clu"), None))
    out_specs = P(("lang", "clu"))

    return jax.shard_map(shards, mesh=mesh, in_specs=in_specs, out_specs=out_specs, check_vma=False)
```

time: 50.9 us -> 47.2 us (0.927)
  blocking collectives: 43.6 us -> 10.9 us
  starting transfers between devices: 0 us -> 17.6 us
  waiting for transfers between devices: 0 us -> 15.4 us
  Pallas kernels: 7.01 us -> 3.01 us
    all_to_all x1 -> x0, blocking collectives: 32.2 us -> none  [shards(): lax.all_to_all(packed, 'clu', split_axis=0, concat_axis=0, tiled=True)]
    ppermute x0 -> x15, starting transfers between devices: none -> 17.6 us  [swap(): return lax.ppermute(array, 'clu', [(i, i ^ k) for i in range(groups)])]
    ppermute x0 -> x15, waiting for transfers between devices: none -> 15.4 us  [swap(): return lax.ppermute(array, 'clu', [(i, i ^ k) for i in range(groups)])]
    pallas_call x3, Pallas kernels: 7.01 us -> 3.01 us  [call(): pl.pallas_call(kernel, out_shape=out_shape, in_specs=in_specs or [VMEM] *...]
  transfers between devices with their start and end apart: 0 -> 15, of which waited for: 0 -> 7; matrix products, arithmetic and copies ran while one was open for 0% -> 0% of each run, Pallas kernels for 0% -> 0%
where the time goes in v2:
time: 47.2 us; the launch traced here: 47 us
  starting transfers between devices  17.6 us (37%)
  waiting for transfers between devices  15.4 us (33%)
  blocking collectives  10.9 us (23%)
  Pallas kernels  3.01 us (6%)
    ppermute x15, starting transfers between devices, swap(): return lax.ppermute(array, 'clu', [(i, i ^ k) for i in range(groups)])  17.6 us
    ppermute x15, waiting for transfers between devices, swap(): return lax.ppermute(array, 'clu', [(i, i ^ k) for i in range(groups)])  15.4 us
    all_to_all x1, blocking collectives, shards(): lax.all_to_all(best, 'clu', split_axis=0, concat_axis=0, tiled=True)  10.9 us
    pallas_call x3, Pallas kernels, call(): pl.pallas_call(kernel, out_shape=out_shape, in_specs=in_specs or [VMEM] *...  3.01 us
  transfers between devices with their start and end apart: 15, of which 7 were waited for; matrix products, arithmetic and copies ran while one was open for 0% of the time, Pallas kernels for 0%

profile of v2, /device:TPU:0, one launch (start us, length us, event | category | flops | bytes accessed | tf_op | source)
XLA Modules:
  0.0 47.0 jit_solution(3654028322509551651)
XLA Ops:
  0.0 1.7 %shard_map.28 = (bf16[32,1024]{1,0:T(8,128)(2,1)S(1)}, bf16[32,1024]{1,0:T(8,128)(2,1)S(1)}, bf16[64,1024]{1,0:T(8,128)(2,1)S(1)}, bf16[64,1024]{1,0:T(8,128)(2,...) custom-call(bf16[256,1024]{1,0:T(8,128)(2,1)} %rows_hbm.1, ...), custom_call_target="tpu_custom_call" | custom-call | flops 16777216 | bytes 1048576 | tf_op jit(solution)/shard_map/pallas_call | solution.py:21
  1.7 2.5 %collective-permute-start.1 = (bf16[64,1024]{1,0:T(8,128)(2,1)S(1)}, bf16[64,1024]{1,0:T(8,128)(2,1)S(1)}, u32[]{:S(2)}, u32[]{:S(2)}) collective-permute-start(bf16[64,1024]{1,0:T(8,128)(2,1)S(1)} %get-tuple-element.19), channel_id=1, source_target_pairs={{0,3},{1,2},{2,1},{3,0},{4,7},{5,6},{6,5},{7,4},{8,11},{9,10},{10,... | collective-permute-start | bytes 393224 | tf_op jit(solution)/shard_map/ppermute | solution.py:165
  4.2 1.9 %collective-permute-start.3 = (bf16[64,1024]{1,0:T(8,128)(2,1)S(1)}, bf16[64,1024]{1,0:T(8,128)(2,1)S(1)}, u32[]{:S(2)}, u32[]{:S(2)}) collective-permute-start(bf16[64,1024]{1,0:T(8,128)(2,1)S(1)} %get-tuple-element.20), channel_id=1, source_target_pairs={{0,5},{1,4},{2,7},{3,6},{4,1},{5,0},{6,3},{7,2},{8,13},{9,12},{10,... | collective-permute-start | bytes 393224 | tf_op jit(solution)/shard_map/ppermute | solution.py:165
  6.0 0.0 collective-permute-start.5
  6.0 3.7 %collective-permute-start.9 = (bf16[64,1024]{1,0:T(8,128)(2,1)S(1)}, bf16[64,1024]{1,0:T(8,128)(2,1)S(1)}, u32[]{:S(2)}, u32[]{:S(2)}) collective-permute-start(bf16[64,1024]{1,0:T(8,128)(2,1)S(1)} %get-tuple-element.24), channel_id=1, source_target_pairs={{0,11},{1,10},{2,9},{3,8},{4,15},{5,14},{6,13},{7,12},{8,3},{9,2},... | collective-permute-start | bytes 393224 | tf_op jit(solution)/shard_map/ppermute | solution.py:165
  9.7 0.8 %collective-permute-start.11 = (bf16[64,1024]{1,0:T(8,128)(2,1)S(1)}, bf16[64,1024]{1,0:T(8,128)(2,1)S(1)}, u32[]{:S(2)}, u32[]{:S(2)}) collective-permute-start(bf16[64,1024]{1,0:T(8,128)(2,1)S(1)} %get-tuple-element.25), channel_id=1, source_target_pairs={{0,13},{1,12},{2,15},{3,14},{4,9},{5,8},{6,11},{7,10},{8,5},{9,4},... | collective-permute-start | bytes 393224 | tf_op jit(solution)/shard_map/ppermute | solution.py:165
  10.5 0.0 collective-permute-done.1.refs_3_
  10.5 2.8 %collective-permute-start.13 = (bf16[64,1024]{1,0:T(8,128)(2,1)S(1)}, bf16[64,1024]{1,0:T(8,128)(2,1)S(1)}, u32[]{:S(2)}, u32[]{:S(2)}) collective-permute-start(bf16[64,1024]{1,0:T(8,128)(2,1)S(1)} %get-tuple-element.26), channel_id=1, source_target_pairs={{0,15},{1,14},{2,13},{3,12},{4,11},{5,10},{6,9},{7,8},{8,7},{9,6},... | collective-permute-start | bytes 393224 | tf_op jit(solution)/shard_map/ppermute | solution.py:165
  13.3 0.0 collective-permute-done.3.refs_5_
  13.3 0.5 collective-permute-start
  13.7 1.8 %collective-permute-done.5.refs_7_ = bf16[64,1024]{1,0:T(8,128)(2,1)S(1)} collective-permute-done((bf16[64,1024]{1,0:T(8,128)(2,1)S(1)}, bf16[64,1024]{1,0:T(8,128)(2,1)S(1)}, u32[]{:S(2)}, u32[]{:S(2)}) %collective-permute-start.5) | collective-permute-done | bytes 131104 | tf_op jit(solution)/shard_map/ppermute | solution.py:165
  15.5 0.9 %collective-permute-start.7 = (bf16[32,1024]{1,0:T(8,128)(2,1)S(1)}, bf16[32,1024]{1,0:T(8,128)(2,1)S(1)}, u32[]{:S(2)}, u32[]{:S(2)}) collective-permute-start(bf16[32,1024]{1,0:T(8,128)(2,1)S(1)} %get-tuple-element.22), channel_id=1, source_target_pairs={{0,8},{1,9},{2,10},{3,11},{4,12},{5,13},{6,14},{7,15},{8,0},{9,1},... | collective-permute-start | bytes 196616 | tf_op jit(solution)/shard_map/ppermute | solution.py:165
  16.4 0.0 collective-permute-done.9.refs_11_
  16.5 2.0 %collective-permute-start.8 = (bf16[32,1024]{1,0:T(8,128)(2,1)S(1)}, bf16[32,1024]{1,0:T(8,128)(2,1)S(1)}, u32[]{:S(2)}, u32[]{:S(2)}) collective-permute-start(bf16[32,1024]{1,0:T(8,128)(2,1)S(1)} %get-tuple-element.23), channel_id=1, source_target_pairs={{0,9},{1,8},{2,11},{3,10},{4,13},{5,12},{6,15},{7,14},{8,1},{9,0},... | collective-permute-start | bytes 196616 | tf_op jit(solution)/shard_map/ppermute | solution.py:165
  18.4 1.5 %collective-permute-done.11.refs_13_ = bf16[64,1024]{1,0:T(8,128)(2,1)S(1)} collective-permute-done((bf16[64,1024]{1,0:T(8,128)(2,1)S(1)}, bf16[64,1024]{1,0:T(8,128)(2,1)S(1)}, u32[]{:S(2)}, u32[]{:S(2)}) %collective-permute-start.11) | collective-permute-done | bytes 131104 | tf_op jit(solution)/shard_map/ppermute | solution.py:165
  19.9 1.5 %collective-permute-start.2 = (bf16[32,1024]{1,0:T(8,128)(2,1)S(1)}, bf16[32,1024]{1,0:T(8,128)(2,1)S(1)}, u32[]{:S(2)}, u32[]{:S(2)}) collective-permute-start(bf16[32,1024]{1,0:T(8,128)(2,1)S(1)} %slice.24), channel_id=1, source_target_pairs={{0,1},{1,0},{2,3},{3,2},{4,5},{5,4},{6,7},{7,6},{8,9},{9,8},{10,11... | collective-permute-start | bytes 196616 | tf_op jit(solution)/shard_map/ppermute | solution.py:165
  21.5 1.8 %collective-permute-done.13.refs_15_ = bf16[64,1024]{1,0:T(8,128)(2,1)S(1)} collective-permute-done((bf16[64,1024]{1,0:T(8,128)(2,1)S(1)}, bf16[64,1024]{1,0:T(8,128)(2,1)S(1)}, u32[]{:S(2)}, u32[]{:S(2)}) %collective-permute-start.13) | collective-permute-done | bytes 131104 | tf_op jit(solution)/shard_map/ppermute | solution.py:165
  23.3 0.1 collective-permute-start.4
  23.4 0.0 collective-permute-done.refs_1_
  23.4 0.5 collective-permute-start.6
  23.9 8.1 %collective-permute-done.7.refs_8_ = bf16[32,1024]{1,0:T(8,128)(2,1)S(1)} collective-permute-done((bf16[32,1024]{1,0:T(8,128)(2,1)S(1)}, bf16[32,1024]{1,0:T(8,128)(2,1)S(1)}, u32[]{:S(2)}, u32[]{:S(2)}) %collective-permute-start.7) | collective-permute-done | bytes 65568 | tf_op jit(solution)/shard_map/ppermute | solution.py:165
  32.0 0.1 collective-permute-start.10
  32.0 1.3 %collective-permute-done.8.refs_9_ = bf16[32,1024]{1,0:T(8,128)(2,1)S(1)} collective-permute-done((bf16[32,1024]{1,0:T(8,128)(2,1)S(1)}, bf16[32,1024]{1,0:T(8,128)(2,1)S(1)}, u32[]{:S(2)}, u32[]{:S(2)}) %collective-permute-start.8) | collective-permute-done | bytes 65568 | tf_op jit(solution)/shard_map/ppermute | solution.py:165
  33.3 0.1 collective-permute-start.12
  33.4 0.0 collective-permute-done.2.refs_2_
  33.4 0.4 collective-permute-start.14
  33.8 0.0 collective-permute-done.4.refs_4_
  33.8 0.0 collective-permute-done.6.refs_6_
  33.8 0.0 collective-permute-done.10.refs_10_
  33.9 0.7 %collective-permute-done.12.refs_12_ = bf16[32,1024]{1,0:T(8,128)(2,1)S(1)} collective-permute-done((bf16[32,1024]{1,0:T(8,128)(2,1)S(1)}, bf16[32,1024]{1,0:T(8,128)(2,1)S(1)}, u32[]{:S(2)}, u32[]{:S(2)}) %collective-permute-start.12) | collective-permute-done | bytes 65568 | tf_op jit(solution)/shard_map/ppermute | solution.py:165
  34.6 0.2 collective-permute-done.14.refs_14_
  34.7 0.5 %shard_map.29 = f32[16,2,128]{2,1,0:T(2,128)S(1)} custom-call(bf16[32,1024]{1,0:T(8,128)(2,1)S(1)} %get-tuple-element.17.refs_0_, bf16[32,1024]{1,0:T(8,128)(2,1)S(1)} %collective-permute-done.refs_1_, bf16[32,1024]{1,0:T(8,128)(2,1)S(1)} %collective-permute-done.2.refs_2_, bf16[64,1024]{1,0:T(8,128)(2,1)S(1)} %collective-permute-done.1.refs_3_, ...), custom_call_target="tpu_custom_call" | custom-call | flops 16777216 | bytes 1048576 | tf_op jit(solution)/shard_map/pallas_call | solution.py:21
  35.2 10.9 %all_to_all.5.best_ref = f32[16,2,128]{2,1,0:T(2,128)S(1)} all-to-all(f32[16,2,128]{2,1,0:T(2,128)S(1)} %shard_map.29), channel_id=1, replica_groups=mesh['lang'=2,'clu'=16] {'clu'}, dimensions={0} | all-to-all | bytes 32768 | tf_op jit(solution)/shard_map/all_to_all | solution.py:232
  46.2 0.8 %shard_map.30 = f32[1,256]{1,0:T(1,128)} custom-call(f32[16,2,128]{2,1,0:T(2,128)S(1)} %all_to_all.5.best_ref, s32[1,256]{1,0:T(1,128)S(1)} %get-tuple-element.27.rank_ref, s32[1,256]{1,0:T(1,128)S(1)} %get-tuple-element.28.cluster_ref), custom_call_target="tpu_custom_call" | custom-call | flops 16777216 | bytes 1048576 | tf_op jit(solution)/shard_map/pallas_call | solution.py:21
  (6 shorter events, 0.0 us)
Async XLA Ops:
  1.7 8.8 %collective-permute-start.1 = (bf16[64,1024]{1,0:T(8,128)(2,1)S(1)}, bf16[64,1024]{1,0:T(8,128)(2,1)S(1)}, u32[]{:S(2)}, u32[]{:S(2)}) collective-permute-start(bf16[64,1024]{1,0:T(8,128)(2,1)S(1)} %get-tuple-element.19), channel_id=1, source_target_pairs={{0,3},{1,2},{2,1},{3,0},{4,7},{5,6},{6,5},{7,4},{8,11},{9,10},{10,... | collective-permute-start | bytes 393224 | tf_op jit(solution)/shard_map/ppermute | solution.py:165
  4.2 9.1 %collective-permute-start.3 = (bf16[64,1024]{1,0:T(8,128)(2,1)S(1)}, bf16[64,1024]{1,0:T(8,128)(2,1)S(1)}, u32[]{:S(2)}, u32[]{:S(2)}) collective-permute-start(bf16[64,1024]{1,0:T(8,128)(2,1)S(1)} %get-tuple-element.20), channel_id=1, source_target_pairs={{0,5},{1,4},{2,7},{3,6},{4,1},{5,0},{6,3},{7,2},{8,13},{9,12},{10,... | collective-permute-start | bytes 393224 | tf_op jit(solution)/shard_map/ppermute | solution.py:165
  6.0 9.5 %collective-permute-start.5 = (bf16[64,1024]{1,0:T(8,128)(2,1)S(1)}, bf16[64,1024]{1,0:T(8,128)(2,1)S(1)}, u32[]{:S(2)}, u32[]{:S(2)}) collective-permute-start(bf16[64,1024]{1,0:T(8,128)(2,1)S(1)} %get-tuple-element.21), channel_id=1, source_target_pairs={{0,7},{1,6},{2,5},{3,4},{4,3},{5,2},{6,1},{7,0},{8,15},{9,14},{10,... | collective-permute-start | bytes 393224 | tf_op jit(solution)/shard_map/ppermute | solution.py:165
  6.0 10.4 %collective-permute-start.9 = (bf16[64,1024]{1,0:T(8,128)(2,1)S(1)}, bf16[64,1024]{1,0:T(8,128)(2,1)S(1)}, u32[]{:S(2)}, u32[]{:S(2)}) collective-permute-start(bf16[64,1024]{1,0:T(8,128)(2,1)S(1)} %get-tuple-element.24), channel_id=1, source_target_pairs={{0,11},{1,10},{2,9},{3,8},{4,15},{5,14},{6,13},{7,12},{8,3},{9,2},... | collective-permute-start | bytes 393224 | tf_op jit(solution)/shard_map/ppermute | solution.py:165
  9.7 10.2 %collective-permute-start.11 = (bf16[64,1024]{1,0:T(8,128)(2,1)S(1)}, bf16[64,1024]{1,0:T(8,128)(2,1)S(1)}, u32[]{:S(2)}, u32[]{:S(2)}) collective-permute-start(bf16[64,1024]{1,0:T(8,128)(2,1)S(1)} %get-tuple-element.25), channel_id=1, source_target_pairs={{0,13},{1,12},{2,15},{3,14},{4,9},{5,8},{6,11},{7,10},{8,5},{9,4},... | collective-permute-start | bytes 393224 | tf_op jit(solution)/shard_map/ppermute | solution.py:165
  10.5 12.8 %collective-permute-start.13 = (bf16[64,1024]{1,0:T(8,128)(2,1)S(1)}, bf16[64,1024]{1,0:T(8,128)(2,1)S(1)}, u32[]{:S(2)}, u32[]{:S(2)}) collective-permute-start(bf16[64,1024]{1,0:T(8,128)(2,1)S(1)} %get-tuple-element.26), channel_id=1, source_target_pairs={{0,15},{1,14},{2,13},{3,12},{4,11},{5,10},{6,9},{7,8},{8,7},{9,6},... | collective-permute-start | bytes 393224 | tf_op jit(solution)/shard_map/ppermute | solution.py:165
  13.3 10.1 %collective-permute-start = (bf16[32,1024]{1,0:T(8,128)(2,1)S(1)}, bf16[32,1024]{1,0:T(8,128)(2,1)S(1)}, u32[]{:S(2)}, u32[]{:S(2)}) collective-permute-start(bf16[32,1024]{1,0:T(8,128)(2,1)S(1)} %get-tuple-element.18), channel_id=1, source_target_pairs={{0,1},{1,0},{2,3},{3,2},{4,5},{5,4},{6,7},{7,6},{8,9},{9,8},{10,11... | collective-permute-start | bytes 196616 | tf_op jit(solution)/shard_map/ppermute | solution.py:165
  15.5 16.4 %collective-permute-start.7 = (bf16[32,1024]{1,0:T(8,128)(2,1)S(1)}, bf16[32,1024]{1,0:T(8,128)(2,1)S(1)}, u32[]{:S(2)}, u32[]{:S(2)}) collective-permute-start(bf16[32,1024]{1,0:T(8,128)(2,1)S(1)} %get-tuple-element.22), channel_id=1, source_target_pairs={{0,8},{1,9},{2,10},{3,11},{4,12},{5,13},{6,14},{7,15},{8,0},{9,1},... | collective-permute-start | bytes 196616 | tf_op jit(solution)/shard_map/ppermute | solution.py:165
  16.5 16.9 %collective-permute-start.8 = (bf16[32,1024]{1,0:T(8,128)(2,1)S(1)}, bf16[32,1024]{1,0:T(8,128)(2,1)S(1)}, u32[]{:S(2)}, u32[]{:S(2)}) collective-permute-start(bf16[32,1024]{1,0:T(8,128)(2,1)S(1)} %get-tuple-element.23), channel_id=1, source_target_pairs={{0,9},{1,8},{2,11},{3,10},{4,13},{5,12},{6,15},{7,14},{8,1},{9,0},... | collective-permute-start | bytes 196616 | tf_op jit(solution)/shard_map/ppermute | solution.py:165
  19.9 13.6 %collective-permute-start.2 = (bf16[32,1024]{1,0:T(8,128)(2,1)S(1)}, bf16[32,1024]{1,0:T(8,128)(2,1)S(1)}, u32[]{:S(2)}, u32[]{:S(2)}) collective-permute-start(bf16[32,1024]{1,0:T(8,128)(2,1)S(1)} %slice.24), channel_id=1, source_target_pairs={{0,1},{1,0},{2,3},{3,2},{4,5},{5,4},{6,7},{7,6},{8,9},{9,8},{10,11... | collective-permute-start | bytes 196616 | tf_op jit(solution)/shard_map/ppermute | solution.py:165
  23.3 10.6 %collective-permute-start.4 = (bf16[32,1024]{1,0:T(8,128)(2,1)S(1)}, bf16[32,1024]{1,0:T(8,128)(2,1)S(1)}, u32[]{:S(2)}, u32[]{:S(2)}) collective-permute-start(bf16[32,1024]{1,0:T(8,128)(2,1)S(1)} %slice.25), channel_id=1, source_target_pairs={{0,1},{1,0},{2,3},{3,2},{4,5},{5,4},{6,7},{7,6},{8,9},{9,8},{10,11... | collective-permute-start | bytes 196616 | tf_op jit(solution)/shard_map/ppermute | solution.py:165
  23.4 10.5 %collective-permute-start.6 = (bf16[32,1024]{1,0:T(8,128)(2,1)S(1)}, bf16[32,1024]{1,0:T(8,128)(2,1)S(1)}, u32[]{:S(2)}, u32[]{:S(2)}) collective-permute-start(bf16[32,1024]{1,0:T(8,128)(2,1)S(1)} %slice.26), channel_id=1, source_target_pairs={{0,1},{1,0},{2,3},{3,2},{4,5},{5,4},{6,7},{7,6},{8,9},{9,8},{10,11... | collective-permute-start | bytes 196616 | tf_op jit(solution)/shard_map/ppermute | solution.py:165
  32.0 1.9 %collective-permute-start.10 = (bf16[32,1024]{1,0:T(8,128)(2,1)S(1)}, bf16[32,1024]{1,0:T(8,128)(2,1)S(1)}, u32[]{:S(2)}, u32[]{:S(2)}) collective-permute-start(bf16[32,1024]{1,0:T(8,128)(2,1)S(1)} %slice.27), channel_id=1, source_target_pairs={{0,1},{1,0},{2,3},{3,2},{4,5},{5,4},{6,7},{7,6},{8,9},{9,8},{10,11... | collective-permute-start | bytes 196616 | tf_op jit(solution)/shard_map/ppermute | solution.py:165
  33.3 1.3 %collective-permute-start.12 = (bf16[32,1024]{1,0:T(8,128)(2,1)S(1)}, bf16[32,1024]{1,0:T(8,128)(2,1)S(1)}, u32[]{:S(2)}, u32[]{:S(2)}) collective-permute-start(bf16[32,1024]{1,0:T(8,128)(2,1)S(1)} %slice.28), channel_id=1, source_target_pairs={{0,1},{1,0},{2,3},{3,2},{4,5},{5,4},{6,7},{7,6},{8,9},{9,8},{10,11... | collective-permute-start | bytes 196616 | tf_op jit(solution)/shard_map/ppermute | solution.py:165
  33.4 1.3 %collective-permute-start.14 = (bf16[32,1024]{1,0:T(8,128)(2,1)S(1)}, bf16[32,1024]{1,0:T(8,128)(2,1)S(1)}, u32[]{:S(2)}, u32[]{:S(2)}) collective-permute-start(bf16[32,1024]{1,0:T(8,128)(2,1)S(1)} %slice.29), channel_id=1, source_target_pairs={{0,1},{1,0},{2,3},{3,2},{4,5},{5,4},{6,7},{7,6},{8,9},{9,8},{10,11... | collective-permute-start | bytes 196616 | tf_op jit(solution)/shard_map/ppermute | solution.py:165

commit v3 on v2

--- a/solution.py
+++ b/solution.py
@@ -95,15 +95,23 @@
 def score_blocks_kernel(most, where, *refs):
     *row_refs, out_ref = refs
     me = lax.axis_index("clu")
+    best = []
     for local in range(CLU_DEV):
         rows = jnp.concatenate(
             [row_refs[n][start + local * most:start + (local + 1) * most] for n, start in where],
             axis=0,
         )
-        best = best_of(rows)
-        for k in range(len(where)):
-            lane = k * most // LANES * LANES
-            out_ref[me ^ k, pl.ds(local, 1), :] = best[:, lane:lane + LANES]
+        best.append(best_of(rows))
+    share = LANES // most
+    group = lax.broadcasted_iota(jnp.int32, (1, LANES), 1) // most
+    for base in range(0, len(where), share):
+        lane = base * most
+        low = best[0][:, lane:lane + LANES]
+        high = pltpu.roll(best[1][:, lane:lane + LANES], most, 1)
+        for parity in range(2):
+            line = jnp.where(group % 2 == parity, low, high)
+            for k in range(base + parity, base + share, 2):
+                out_ref[me ^ k] = line
 
 
 def score_all_kernel(most, rows_ref, out_ref):
@@ -115,28 +123,26 @@
 
 
 def pick_kernel(most, relative, best_ref, rank_ref, cluster_ref, out_ref):
-    groups, lines = best_ref.shape[:2]
+    groups = best_ref.shape[0]
     count = rank_ref.shape[1]
     me = lax.axis_index("clu")
     cluster = cluster_ref[...]
     owner = cluster // CLU_DEV
     local = cluster % CLU_DEV
     if relative:
-        lane = (owner ^ me) * most + rank_ref[...]
+        lane = ((owner ^ me) + local) * most + rank_ref[...]
     else:
         lane = (me * CLU_DEV + local) * most + rank_ref[...]
-    inner = (lax.broadcasted_iota(jnp.int32, (LANES, count), 0) == lane % LANES).astype(jnp.float32)
-    total = jnp.zeros((1, count), jnp.float32)
-    for line in range(lines):
-        table = jnp.dot(
-            best_ref[:, line, :], inner, precision=lax.Precision.HIGHEST,
-            preferred_element_type=jnp.float32,
+    lane = lane % LANES
+    best = best_ref[:, 0, :]
+    row = lax.broadcasted_iota(jnp.int32, (groups, LANES), 0)
+    for start in range(0, count, LANES):
+        index = jnp.broadcast_to(lane[:, start:start + LANES], (groups, LANES))
+        table = jnp.take_along_axis(best, index, axis=1)
+        mine = row == owner[:, start:start + LANES]
+        out_ref[:, start:start + LANES] = jnp.sum(
+            jnp.where(mine, table, 0.0), axis=0, keepdims=True
         )
-        outer = lax.broadcasted_iota(jnp.int32, (groups, count), 0) == owner
-        if lines > 1:
-            outer &= local == line
-        total += jnp.sum(jnp.where(outer, table, 0.0), axis=0, keepdims=True)
-    out_ref[...] = total
 
 
 def pack(embeddings, assignment, sizes, most, labels, relative):
@@ -196,7 +202,7 @@
             where += [(len(args) - 2, 0), (len(args) - 1, 0)]
     best = call(
         functools.partial(score_blocks_kernel, most, tuple(where)),
-        jax.ShapeDtypeStruct((groups, CLU_DEV, LANES), jnp.float32), args,
+        jax.ShapeDtypeStruct((groups, 1, LANES), jnp.float32), args,
     )
     return best, rank, cluster
 
@@ -218,7 +224,8 @@
 
 
 def uses_blocks(groups, most):
-    return most % 16 == 0 and groups >= 4 and groups & (groups - 1) == 0
+    power = groups & (groups - 1) == 0
+    return power and groups >= 16 and most % 16 == 0 and LANES % (2 * most) == 0
 
 
 def shards(embeddings, assignment):

time: 47.2 us -> 47 us (level)
  no operation moved by 1% of the time
where the time goes in v3:
time: 47 us; the launch traced here: 46.8 us
  starting transfers between devices  17.6 us (37%)
  waiting for transfers between devices  15.4 us (33%)
  blocking collectives  10.9 us (23%)
  Pallas kernels  2.92 us (6%)
    ppermute x15, starting transfers between devices, swap(): return lax.ppermute(array, 'clu', [(i, i ^ k) for i in range(groups)])  17.6 us
    ppermute x15, waiting for transfers between devices, swap(): return lax.ppermute(array, 'clu', [(i, i ^ k) for i in range(groups)])  15.4 us
    all_to_all x1, blocking collectives, shards(): lax.all_to_all(best, 'clu', split_axis=0, concat_axis=0, tiled=True)  10.9 us
    pallas_call x3, Pallas kernels, call(): pl.pallas_call(kernel, out_shape=out_shape, in_specs=in_specs or [VMEM] *...  2.92 us
  transfers between devices with their start and end apart: 15, of which 7 were waited for; matrix products, arithmetic and copies ran while one was open for 0% of the time, Pallas kernels for 0%

profile of v3, /device:TPU:0, one launch (start us, length us, event | category | flops | bytes accessed | tf_op | source)
XLA Modules:
  0.0 46.8 jit_solution(9516842577499206804)
XLA Ops:
  0.0 1.7 %shard_map.28 = (bf16[32,1024]{1,0:T(8,128)(2,1)S(1)}, bf16[32,1024]{1,0:T(8,128)(2,1)S(1)}, bf16[64,1024]{1,0:T(8,128)(2,1)S(1)}, bf16[64,1024]{1,0:T(8,128)(2,...) custom-call(bf16[256,1024]{1,0:T(8,128)(2,1)} %rows_hbm.1, ...), custom_call_target="tpu_custom_call" | custom-call | flops 16777216 | bytes 1048576 | tf_op jit(solution)/shard_map/pallas_call | solution.py:21
  1.7 2.5 %collective-permute-start.1 = (bf16[64,1024]{1,0:T(8,128)(2,1)S(1)}, bf16[64,1024]{1,0:T(8,128)(2,1)S(1)}, u32[]{:S(2)}, u32[]{:S(2)}) collective-permute-start(bf16[64,1024]{1,0:T(8,128)(2,1)S(1)} %get-tuple-element.19), channel_id=1, source_target_pairs={{0,3},{1,2},{2,1},{3,0},{4,7},{5,6},{6,5},{7,4},{8,11},{9,10},{10,... | collective-permute-start | bytes 393224 | tf_op jit(solution)/shard_map/ppermute | solution.py:171
  4.2 1.9 %collective-permute-start.3 = (bf16[64,1024]{1,0:T(8,128)(2,1)S(1)}, bf16[64,1024]{1,0:T(8,128)(2,1)S(1)}, u32[]{:S(2)}, u32[]{:S(2)}) collective-permute-start(bf16[64,1024]{1,0:T(8,128)(2,1)S(1)} %get-tuple-element.20), channel_id=1, source_target_pairs={{0,5},{1,4},{2,7},{3,6},{4,1},{5,0},{6,3},{7,2},{8,13},{9,12},{10,... | collective-permute-start | bytes 393224 | tf_op jit(solution)/shard_map/ppermute | solution.py:171
  6.0 0.0 collective-permute-start.5
  6.0 3.7 %collective-permute-start.9 = (bf16[64,1024]{1,0:T(8,128)(2,1)S(1)}, bf16[64,1024]{1,0:T(8,128)(2,1)S(1)}, u32[]{:S(2)}, u32[]{:S(2)}) collective-permute-start(bf16[64,1024]{1,0:T(8,128)(2,1)S(1)} %get-tuple-element.24), channel_id=1, source_target_pairs={{0,11},{1,10},{2,9},{3,8},{4,15},{5,14},{6,13},{7,12},{8,3},{9,2},... | collective-permute-start | bytes 393224 | tf_op jit(solution)/shard_map/ppermute | solution.py:171
  9.7 0.8 %collective-permute-start.11 = (bf16[64,1024]{1,0:T(8,128)(2,1)S(1)}, bf16[64,1024]{1,0:T(8,128)(2,1)S(1)}, u32[]{:S(2)}, u32[]{:S(2)}) collective-permute-start(bf16[64,1024]{1,0:T(8,128)(2,1)S(1)} %get-tuple-element.25), channel_id=1, source_target_pairs={{0,13},{1,12},{2,15},{3,14},{4,9},{5,8},{6,11},{7,10},{8,5},{9,4},... | collective-permute-start | bytes 393224 | tf_op jit(solution)/shard_map/ppermute | solution.py:171
  10.5 0.0 collective-permute-done.1.refs_3_
  10.5 2.8 %collective-permute-start.13 = (bf16[64,1024]{1,0:T(8,128)(2,1)S(1)}, bf16[64,1024]{1,0:T(8,128)(2,1)S(1)}, u32[]{:S(2)}, u32[]{:S(2)}) collective-permute-start(bf16[64,1024]{1,0:T(8,128)(2,1)S(1)} %get-tuple-element.26), channel_id=1, source_target_pairs={{0,15},{1,14},{2,13},{3,12},{4,11},{5,10},{6,9},{7,8},{8,7},{9,6},... | collective-permute-start | bytes 393224 | tf_op jit(solution)/shard_map/ppermute | solution.py:171
  13.3 0.0 collective-permute-done.3.refs_5_
  13.3 0.5 collective-permute-start
  13.7 1.8 %collective-permute-done.5.refs_7_ = bf16[64,1024]{1,0:T(8,128)(2,1)S(1)} collective-permute-done((bf16[64,1024]{1,0:T(8,128)(2,1)S(1)}, bf16[64,1024]{1,0:T(8,128)(2,1)S(1)}, u32[]{:S(2)}, u32[]{:S(2)}) %collective-permute-start.5) | collective-permute-done | bytes 131104 | tf_op jit(solution)/shard_map/ppermute | solution.py:171
  15.5 0.9 %collective-permute-start.7 = (bf16[32,1024]{1,0:T(8,128)(2,1)S(1)}, bf16[32,1024]{1,0:T(8,128)(2,1)S(1)}, u32[]{:S(2)}, u32[]{:S(2)}) collective-permute-start(bf16[32,1024]{1,0:T(8,128)(2,1)S(1)} %get-tuple-element.22), channel_id=1, source_target_pairs={{0,8},{1,9},{2,10},{3,11},{4,12},{5,13},{6,14},{7,15},{8,0},{9,1},... | collective-permute-start | bytes 196616 | tf_op jit(solution)/shard_map/ppermute | solution.py:171
  16.4 0.0 collective-permute-done.9.refs_11_
  16.5 2.0 %collective-permute-start.8 = (bf16[32,1024]{1,0:T(8,128)(2,1)S(1)}, bf16[32,1024]{1,0:T(8,128)(2,1)S(1)}, u32[]{:S(2)}, u32[]{:S(2)}) collective-permute-start(bf16[32,1024]{1,0:T(8,128)(2,1)S(1)} %get-tuple-element.23), channel_id=1, source_target_pairs={{0,9},{1,8},{2,11},{3,10},{4,13},{5,12},{6,15},{7,14},{8,1},{9,0},... | collective-permute-start | bytes 196616 | tf_op jit(solution)/shard_map/ppermute | solution.py:171
  18.4 1.5 %collective-permute-done.11.refs_13_ = bf16[64,1024]{1,0:T(8,128)(2,1)S(1)} collective-permute-done((bf16[64,1024]{1,0:T(8,128)(2,1)S(1)}, bf16[64,1024]{1,0:T(8,128)(2,1)S(1)}, u32[]{:S(2)}, u32[]{:S(2)}) %collective-permute-start.11) | collective-permute-done | bytes 131104 | tf_op jit(solution)/shard_map/ppermute | solution.py:171
  19.9 1.5 %collective-permute-start.2 = (bf16[32,1024]{1,0:T(8,128)(2,1)S(1)}, bf16[32,1024]{1,0:T(8,128)(2,1)S(1)}, u32[]{:S(2)}, u32[]{:S(2)}) collective-permute-start(bf16[32,1024]{1,0:T(8,128)(2,1)S(1)} %slice.24), channel_id=1, source_target_pairs={{0,1},{1,0},{2,3},{3,2},{4,5},{5,4},{6,7},{7,6},{8,9},{9,8},{10,11... | collective-permute-start | bytes 196616 | tf_op jit(solution)/shard_map/ppermute | solution.py:171
  21.5 1.8 %collective-permute-done.13.refs_15_ = bf16[64,1024]{1,0:T(8,128)(2,1)S(1)} collective-permute-done((bf16[64,1024]{1,0:T(8,128)(2,1)S(1)}, bf16[64,1024]{1,0:T(8,128)(2,1)S(1)}, u32[]{:S(2)}, u32[]{:S(2)}) %collective-permute-start.13) | collective-permute-done | bytes 131104 | tf_op jit(solution)/shard_map/ppermute | solution.py:171
  23.3 0.1 collective-permute-start.4
  23.4 0.0 collective-permute-done.refs_1_
  23.4 0.5 collective-permute-start.6
  23.9 8.1 %collective-permute-done.7.refs_8_ = bf16[32,1024]{1,0:T(8,128)(2,1)S(1)} collective-permute-done((bf16[32,1024]{1,0:T(8,128)(2,1)S(1)}, bf16[32,1024]{1,0:T(8,128)(2,1)S(1)}, u32[]{:S(2)}, u32[]{:S(2)}) %collective-permute-start.7) | collective-permute-done | bytes 65568 | tf_op jit(solution)/shard_map/ppermute | solution.py:171
  32.0 0.1 collective-permute-start.10
  32.0 1.3 %collective-permute-done.8.refs_9_ = bf16[32,1024]{1,0:T(8,128)(2,1)S(1)} collective-permute-done((bf16[32,1024]{1,0:T(8,128)(2,1)S(1)}, bf16[32,1024]{1,0:T(8,128)(2,1)S(1)}, u32[]{:S(2)}, u32[]{:S(2)}) %collective-permute-start.8) | collective-permute-done | bytes 65568 | tf_op jit(solution)/shard_map/ppermute | solution.py:171
  33.3 0.1 collective-permute-start.12
  33.4 0.0 collective-permute-done.2.refs_2_
  33.4 0.4 collective-permute-start.14
  33.8 0.0 collective-permute-done.4.refs_4_
  33.8 0.0 collective-permute-done.6.refs_6_
  33.8 0.0 collective-permute-done.10.refs_10_
  33.9 0.7 %collective-permute-done.12.refs_12_ = bf16[32,1024]{1,0:T(8,128)(2,1)S(1)} collective-permute-done((bf16[32,1024]{1,0:T(8,128)(2,1)S(1)}, bf16[32,1024]{1,0:T(8,128)(2,1)S(1)}, u32[]{:S(2)}, u32[]{:S(2)}) %collective-permute-start.12) | collective-permute-done | bytes 65568 | tf_op jit(solution)/shard_map/ppermute | solution.py:171
  34.6 0.2 collective-permute-done.14.refs_14_
  34.7 0.6 %shard_map.29 = f32[16,1,128]{2,1,0:T(1,128)S(1)} custom-call(bf16[32,1024]{1,0:T(8,128)(2,1)S(1)} %get-tuple-element.17.refs_0_, bf16[32,1024]{1,0:T(8,128)(2,1)S(1)} %collective-permute-done.refs_1_, bf16[32,1024]{1,0:T(8,128)(2,1)S(1)} %collective-permute-done.2.refs_2_, bf16[64,1024]{1,0:T(8,128)(2,1)S(1)} %collective-permute-done.1.refs_3_, ...), custom_call_target="tpu_custom_call" | custom-call | flops 16777216 | bytes 1048576 | tf_op jit(solution)/shard_map/pallas_call | solution.py:21
  35.3 10.9 %all_to_all.5.best_ref = f32[16,1,128]{2,1,0:T(1,128)S(1)} all-to-all(f32[16,1,128]{2,1,0:T(1,128)S(1)} %shard_map.29), channel_id=1, replica_groups=mesh['lang'=2,'clu'=16] {'clu'}, dimensions={0} | all-to-all | bytes 16384 | tf_op jit(solution)/shard_map/all_to_all | solution.py:239
  46.2 0.7 %shard_map.30 = f32[1,256]{1,0:T(1,128)} custom-call(f32[16,1,128]{2,1,0:T(1,128)S(1)} %all_to_all.5.best_ref, s32[1,256]{1,0:T(1,128)S(1)} %get-tuple-element.27.rank_ref, s32[1,256]{1,0:T(1,128)S(1)} %get-tuple-element.28.cluster_ref), custom_call_target="tpu_custom_call" | custom-call | flops 16777216 | bytes 1048576 | tf_op jit(solution)/shard_map/pallas_call | solution.py:21
  (6 shorter events, 0.0 us)
Async XLA Ops:
  1.7 8.8 %collective-permute-start.1 = (bf16[64,1024]{1,0:T(8,128)(2,1)S(1)}, bf16[64,1024]{1,0:T(8,128)(2,1)S(1)}, u32[]{:S(2)}, u32[]{:S(2)}) collective-permute-start(bf16[64,1024]{1,0:T(8,128)(2,1)S(1)} %get-tuple-element.19), channel_id=1, source_target_pairs={{0,3},{1,2},{2,1},{3,0},{4,7},{5,6},{6,5},{7,4},{8,11},{9,10},{10,... | collective-permute-start | bytes 393224 | tf_op jit(solution)/shard_map/ppermute | solution.py:171
  4.2 9.1 %collective-permute-start.3 = (bf16[64,1024]{1,0:T(8,128)(2,1)S(1)}, bf16[64,1024]{1,0:T(8,128)(2,1)S(1)}, u32[]{:S(2)}, u32[]{:S(2)}) collective-permute-start(bf16[64,1024]{1,0:T(8,128)(2,1)S(1)} %get-tuple-element.20), channel_id=1, source_target_pairs={{0,5},{1,4},{2,7},{3,6},{4,1},{5,0},{6,3},{7,2},{8,13},{9,12},{10,... | collective-permute-start | bytes 393224 | tf_op jit(solution)/shard_map/ppermute | solution.py:171
  6.0 9.5 %collective-permute-start.5 = (bf16[64,1024]{1,0:T(8,128)(2,1)S(1)}, bf16[64,1024]{1,0:T(8,128)(2,1)S(1)}, u32[]{:S(2)}, u32[]{:S(2)}) collective-permute-start(bf16[64,1024]{1,0:T(8,128)(2,1)S(1)} %get-tuple-element.21), channel_id=1, source_target_pairs={{0,7},{1,6},{2,5},{3,4},{4,3},{5,2},{6,1},{7,0},{8,15},{9,14},{10,... | collective-permute-start | bytes 393224 | tf_op jit(solution)/shard_map/ppermute | solution.py:171
  6.0 10.4 %collective-permute-start.9 = (bf16[64,1024]{1,0:T(8,128)(2,1)S(1)}, bf16[64,1024]{1,0:T(8,128)(2,1)S(1)}, u32[]{:S(2)}, u32[]{:S(2)}) collective-permute-start(bf16[64,1024]{1,0:T(8,128)(2,1)S(1)} %get-tuple-element.24), channel_id=1, source_target_pairs={{0,11},{1,10},{2,9},{3,8},{4,15},{5,14},{6,13},{7,12},{8,3},{9,2},... | collective-permute-start | bytes 393224 | tf_op jit(solution)/shard_map/ppermute | solution.py:171
  9.7 10.2 %collective-permute-start.11 = (bf16[64,1024]{1,0:T(8,128)(2,1)S(1)}, bf16[64,1024]{1,0:T(8,128)(2,1)S(1)}, u32[]{:S(2)}, u32[]{:S(2)}) collective-permute-start(bf16[64,1024]{1,0:T(8,128)(2,1)S(1)} %get-tuple-element.25), channel_id=1, source_target_pairs={{0,13},{1,12},{2,15},{3,14},{4,9},{5,8},{6,11},{7,10},{8,5},{9,4},... | collective-permute-start | bytes 393224 | tf_op jit(solution)/shard_map/ppermute | solution.py:171
  10.5 12.8 %collective-permute-start.13 = (bf16[64,1024]{1,0:T(8,128)(2,1)S(1)}, bf16[64,1024]{1,0:T(8,128)(2,1)S(1)}, u32[]{:S(2)}, u32[]{:S(2)}) collective-permute-start(bf16[64,1024]{1,0:T(8,128)(2,1)S(1)} %get-tuple-element.26), channel_id=1, source_target_pairs={{0,15},{1,14},{2,13},{3,12},{4,11},{5,10},{6,9},{7,8},{8,7},{9,6},... | collective-permute-start | bytes 393224 | tf_op jit(solution)/shard_map/ppermute | solution.py:171
  13.3 10.1 %collective-permute-start = (bf16[32,1024]{1,0:T(8,128)(2,1)S(1)}, bf16[32,1024]{1,0:T(8,128)(2,1)S(1)}, u32[]{:S(2)}, u32[]{:S(2)}) collective-permute-start(bf16[32,1024]{1,0:T(8,128)(2,1)S(1)} %get-tuple-element.18), channel_id=1, source_target_pairs={{0,1},{1,0},{2,3},{3,2},{4,5},{5,4},{6,7},{7,6},{8,9},{9,8},{10,11... | collective-permute-start | bytes 196616 | tf_op jit(solution)/shard_map/ppermute | solution.py:171
  15.5 16.4 %collective-permute-start.7 = (bf16[32,1024]{1,0:T(8,128)(2,1)S(1)}, bf16[32,1024]{1,0:T(8,128)(2,1)S(1)}, u32[]{:S(2)}, u32[]{:S(2)}) collective-permute-start(bf16[32,1024]{1,0:T(8,128)(2,1)S(1)} %get-tuple-element.22), channel_id=1, source_target_pairs={{0,8},{1,9},{2,10},{3,11},{4,12},{5,13},{6,14},{7,15},{8,0},{9,1},... | collective-permute-start | bytes 196616 | tf_op jit(solution)/shard_map/ppermute | solution.py:171
  16.5 16.9 %collective-permute-start.8 = (bf16[32,1024]{1,0:T(8,128)(2,1)S(1)}, bf16[32,1024]{1,0:T(8,128)(2,1)S(1)}, u32[]{:S(2)}, u32[]{:S(2)}) collective-permute-start(bf16[32,1024]{1,0:T(8,128)(2,1)S(1)} %get-tuple-element.23), channel_id=1, source_target_pairs={{0,9},{1,8},{2,11},{3,10},{4,13},{5,12},{6,15},{7,14},{8,1},{9,0},... | collective-permute-start | bytes 196616 | tf_op jit(solution)/shard_map/ppermute | solution.py:171
  19.9 13.6 %collective-permute-start.2 = (bf16[32,1024]{1,0:T(8,128)(2,1)S(1)}, bf16[32,1024]{1,0:T(8,128)(2,1)S(1)}, u32[]{:S(2)}, u32[]{:S(2)}) collective-permute-start(bf16[32,1024]{1,0:T(8,128)(2,1)S(1)} %slice.24), channel_id=1, source_target_pairs={{0,1},{1,0},{2,3},{3,2},{4,5},{5,4},{6,7},{7,6},{8,9},{9,8},{10,11... | collective-permute-start | bytes 196616 | tf_op jit(solution)/shard_map/ppermute | solution.py:171
  23.3 10.6 %collective-permute-start.4 = (bf16[32,1024]{1,0:T(8,128)(2,1)S(1)}, bf16[32,1024]{1,0:T(8,128)(2,1)S(1)}, u32[]{:S(2)}, u32[]{:S(2)}) collective-permute-start(bf16[32,1024]{1,0:T(8,128)(2,1)S(1)} %slice.25), channel_id=1, source_target_pairs={{0,1},{1,0},{2,3},{3,2},{4,5},{5,4},{6,7},{7,6},{8,9},{9,8},{10,11... | collective-permute-start | bytes 196616 | tf_op jit(solution)/shard_map/ppermute | solution.py:171
  23.4 10.5 %collective-permute-start.6 = (bf16[32,1024]{1,0:T(8,128)(2,1)S(1)}, bf16[32,1024]{1,0:T(8,128)(2,1)S(1)}, u32[]{:S(2)}, u32[]{:S(2)}) collective-permute-start(bf16[32,1024]{1,0:T(8,128)(2,1)S(1)} %slice.26), channel_id=1, source_target_pairs={{0,1},{1,0},{2,3},{3,2},{4,5},{5,4},{6,7},{7,6},{8,9},{9,8},{10,11... | collective-permute-start | bytes 196616 | tf_op jit(solution)/shard_map/ppermute | solution.py:171
  32.0 1.9 %collective-permute-start.10 = (bf16[32,1024]{1,0:T(8,128)(2,1)S(1)}, bf16[32,1024]{1,0:T(8,128)(2,1)S(1)}, u32[]{:S(2)}, u32[]{:S(2)}) collective-permute-start(bf16[32,1024]{1,0:T(8,128)(2,1)S(1)} %slice.27), channel_id=1, source_target_pairs={{0,1},{1,0},{2,3},{3,2},{4,5},{5,4},{6,7},{7,6},{8,9},{9,8},{10,11... | collective-permute-start | bytes 196616 | tf_op jit(solution)/shard_map/ppermute | solution.py:171
  33.3 1.3 %collective-permute-start.12 = (bf16[32,1024]{1,0:T(8,128)(2,1)S(1)}, bf16[32,1024]{1,0:T(8,128)(2,1)S(1)}, u32[]{:S(2)}, u32[]{:S(2)}) collective-permute-start(bf16[32,1024]{1,0:T(8,128)(2,1)S(1)} %slice.28), channel_id=1, source_target_pairs={{0,1},{1,0},{2,3},{3,2},{4,5},{5,4},{6,7},{7,6},{8,9},{9,8},{10,11... | collective-permute-start | bytes 196616 | tf_op jit(solution)/shard_map/ppermute | solution.py:171
  33.4 1.3 %collective-permute-start.14 = (bf16[32,1024]{1,0:T(8,128)(2,1)S(1)}, bf16[32,1024]{1,0:T(8,128)(2,1)S(1)}, u32[]{:S(2)}, u32[]{:S(2)}) collective-permute-start(bf16[32,1024]{1,0:T(8,128)(2,1)S(1)} %slice.29), channel_id=1, source_target_pairs={{0,1},{1,0},{2,3},{3,2},{4,5},{5,4},{6,7},{7,6},{8,9},{9,8},{10,11... | collective-permute-start | bytes 196616 | tf_op jit(solution)/shard_map/ppermute | solution.py:171

commit v4 on v3

v4 whole, which is shorter than its diff:
```python
import functools

import jax
import jax.numpy as jnp
from jax import lax
from jax.experimental import pallas as pl
from jax.experimental.pallas import tpu as pltpu
from jax.sharding import PartitionSpec as P


CLU_DEV = 2
EPS = 1e-06
PAD = 2.0
RAW_PAD = 64.0
LANES = 128
GRANT = 12 * 1024 * 1024
VMEM = pl.BlockSpec(memory_space=pltpu.VMEM)
HBM = pl.BlockSpec(memory_space=pltpu.HBM)


def call(kernel, out_shape, args, in_specs=None, scratch=(), flops=1 << 24, grant=GRANT):
    return pl.pallas_call(
        kernel,
        out_shape=out_shape,
        in_specs=in_specs or [VMEM] * len(args),
        out_specs=jax.tree.map(lambda _: VMEM, out_shape),
        scratch_shapes=scratch,
        compiler_params=pltpu.CompilerParams(vmem_limit_bytes=grant),
        cost_estimate=pl.CostEstimate(flops=flops, bytes_accessed=1 << 20, transcendentals=0),
    )(*args)


def rank_of(cluster, labels):
    count = cluster.shape[1]
    member = lax.broadcasted_iota(jnp.int32, (labels, count), 0) == cluster
    before = (
        lax.broadcasted_iota(jnp.int32, (count, count), 0)
        < lax.broadcasted_iota(jnp.int32, (count, count), 1)
    ).astype(jnp.bfloat16)
    prior = jnp.dot(member.astype(jnp.bfloat16), before, preferred_element_type=jnp.float32)
    return jnp.sum(jnp.where(member, prior, 0.0), axis=0, keepdims=True).astype(jnp.int32)


def unit_rows(rows):
    values = rows.astype(jnp.float32)
    scale = lax.rsqrt(jnp.sum(values * values, axis=-1, keepdims=True) + EPS)
    return (values * scale).astype(jnp.bfloat16)


def place_rows(first, sizes, position, rows, pad, out_refs):
    slots = sum(sizes)
    count = rows.shape[0]
    place = lax.broadcasted_iota(jnp.int32, (slots, count), 0) + first == position
    live = jnp.sum(place.astype(jnp.float32), axis=1, keepdims=True) > 0
    packed = jnp.dot(place.astype(jnp.bfloat16), rows, preferred_element_type=jnp.float32)
    column = lax.broadcasted_iota(jnp.int32, (slots, LANES), 1) == 0
    head = jnp.where(column & ~live, pad, packed[:, :LANES]).astype(jnp.bfloat16)
    rest = packed[:, LANES:].astype(jnp.bfloat16)
    start = 0
    for size, out_ref in zip(sizes, out_refs):
        out_ref[:, :LANES] = head[start:start + size]
        out_ref[:, LANES:] = rest[start:start + size]
        start += size


def pack_kernel(sizes, most, labels, block_of, rows_hbm, cluster_hbm, *refs):
    *out_refs, rows_ref, position_ref, rank_ref, cluster_ref, sems = refs
    load_cluster = pltpu.make_async_copy(cluster_hbm, cluster_ref, sems.at[0])
    load_rows = pltpu.make_async_copy(rows_hbm, rows_ref, sems.at[1])
    load_cluster.start()
    load_rows.start()
    load_cluster.wait()
    cluster = cluster_ref[...]
    rank = rank_of(cluster, labels)
    rank_ref[...] = rank
    owner = block_of(cluster // CLU_DEV)
    position = (owner * CLU_DEV + cluster % CLU_DEV) * most + rank
    position_ref[...] = position
    load_rows.wait()
    place_rows(0, sizes, position, rows_ref[...], RAW_PAD, out_refs)


def pack_rest_kernel(first, sizes, rows_ref, position_ref, *out_refs):
    place_rows(first, sizes, position_ref[...], unit_rows(rows_ref[...]), PAD, out_refs)


def fits(rows, limit):
    return rows[:, :1].astype(jnp.float32) < limit


def marked_units(rows):
    live = fits(rows, RAW_PAD / 2)
    unit = unit_rows(rows)
    column = lax.broadcasted_iota(jnp.int32, (rows.shape[0], LANES), 1) == 0
    head = jnp.where(column & ~live, PAD, unit[:, :LANES].astype(jnp.float32))
    return jnp.concatenate([head.astype(jnp.bfloat16), unit[:, LANES:]], axis=1)


def best_over(left, right, offset, keep=None):
    gram = lax.dot_general(
        left, right, (((1,), (1,)), ((), ())), preferred_element_type=jnp.float32
    )
    i = lax.broadcasted_iota(jnp.int32, gram.shape, 0)
    j = lax.broadcasted_iota(jnp.int32, gram.shape, 1)
    mask = fits(left, PAD * 0.75) & (i + offset != j)
    if keep is not None:
        mask &= keep(i, j)
    return jnp.max(jnp.where(mask, gram, -1.0), axis=0, keepdims=True)


def units_kernel(*refs):
    half = len(refs) // 2
    for row_ref, out_ref in zip(refs[:half], refs[half:]):
        out_ref[...] = marked_units(row_ref[:out_ref.shape[0]])


def score_blocks_kernel(most, where, *refs):
    *row_refs, out_ref = refs
    me = lax.axis_index("clu")
    best = []
    for local in range(CLU_DEV):
        rows = jnp.concatenate(
            [row_refs[n][start + local * most:start + (local + 1) * most] for n, start in where],
            axis=0,
        )
        best.append(best_over(rows, rows, 0))
    share = LANES // most
    group = lax.broadcasted_iota(jnp.int32, (1, LANES), 1) // most
    for base in range(0, len(where), share):
        lane = base * most
        low = best[0][:, lane:lane + LANES]
        high = pltpu.roll(best[1][:, lane:lane + LANES], most, 1)
        for parity in range(2):
            line = jnp.where(group % 2 == parity, low, high)
            for k in range(base + parity, base + share, 2):
                out_ref[me ^ k] = line


def score_all_kernel(most, rows_ref, out_ref):
    groups = out_ref.shape[0]
    units = marked_units(rows_ref[...])
    best = best_over(units, units, 0, lambda i, j: ((i // most) ^ (j // most)) % CLU_DEV == 0)
    share = LANES // (CLU_DEV * most)
    for p in range(groups):
        out_ref[p] = best[:, p // share * LANES:(p // share + 1) * LANES]


def pick_kernel(most, relative, best_ref, rank_ref, cluster_ref, out_ref):
    groups = best_ref.shape[0]
    count = rank_ref.shape[1]
    me = lax.axis_index("clu")
    cluster = cluster_ref[...]
    owner = cluster // CLU_DEV
    local = cluster % CLU_DEV
    if relative:
        lane = ((owner ^ me) + local) * most + rank_ref[...]
    else:
        lane = (me * CLU_DEV + local) * most + rank_ref[...]
    lane = lane % LANES
    best = best_ref[:, 0, :]
    row = lax.broadcasted_iota(jnp.int32, (groups, LANES), 0)
    for start in range(0, count, LANES):
        index = jnp.broadcast_to(lane[:, start:start + LANES], (groups, LANES))
        table = jnp.take_along_axis(best, index, axis=1)
        mine = row == owner[:, start:start + LANES]
        out_ref[:, start:start + LANES] = jnp.sum(
            jnp.where(mine, table, 0.0), axis=0, keepdims=True
        )


def pack(embeddings, assignment, sizes, most, labels, block_of):
    count, width = embeddings.shape
    line = jax.ShapeDtypeStruct((1, count), jnp.int32)
    rows = jax.ShapeDtypeStruct((count, width), jnp.bfloat16)
    out = tuple(jax.ShapeDtypeStruct((size, width), jnp.bfloat16) for size in sizes)
    *packed, rows, position, rank, cluster = call(
        functools.partial(pack_kernel, sizes, most, labels, block_of),
        (*out, rows, line, line, line),
        (
            pltpu.with_memory_space_constraint(embeddings, pltpu.HBM),
            pltpu.with_memory_space_constraint(assignment.reshape(1, count), pltpu.HBM),
        ),
        in_specs=[HBM, HBM],
        scratch=[pltpu.SemaphoreType.DMA((2,))],
    )
    return packed, rows, position, rank, cluster


def swap(array, k):
    groups = lax.axis_size("clu")
    return lax.ppermute(array, "clu", [(i, i ^ k) for i in range(groups)])


def message_order(groups):
    chips = groups // 2
    last = chips // 2
    far = [2 * m + 1 for m in range(chips - 1, last - 1, -1)]
    near = [2 * m + 1 for m in range(last - 1, 0, -1)]
    return [*far, near[-1], 2 * last, *near[:-1], 1]


def exchange_blocks(embeddings, assignment, most, labels):
    groups = lax.axis_size("clu")
    width = embeddings.shape[1]
    block = CLU_DEV * most
    last = groups // 2
    order = message_order(groups)
    held = [[k] if k in (last, last + 1, 1) else [k, k - 1] for k in order] + [[0]]
    flat = [k for blocks in held for k in blocks]
    sizes = [block * len(blocks) for blocks in held]

    def block_of(owner):
        k = owner ^ lax.axis_index("clu")
        spot = jnp.zeros_like(k)
        for n, value in enumerate(flat):
            spot = jnp.where(k == value, n, spot)
        return spot

    ahead = 2
    packed, rows, position, rank, cluster = pack(
        embeddings, assignment, tuple(sizes[:ahead]), most, labels, block_of
    )
    packed = [*packed, *call(
        functools.partial(pack_rest_kernel, sum(sizes[:ahead]), tuple(sizes[ahead:])),
        tuple(jax.ShapeDtypeStruct((size, width), jnp.bfloat16) for size in sizes[ahead:]),
        (rows, position),
    )]
    spots = {0: (packed[-1], 0)}
    for k, message in zip(order, packed):
        arrived = swap(message, k)
        spots[k] = arrived, 0
        if message.shape[0] > block:
            spots[k - 1] = swap(arrived[block:], 1), 0
    raw = [k for blocks in held[:ahead] for k in blocks]
    units = call(
        units_kernel,
        tuple(jax.ShapeDtypeStruct((block, width), jnp.bfloat16) for _ in raw),
        tuple(spots[k][0] for k in raw),
    )
    spots.update((k, (unit, 0)) for k, unit in zip(raw, units))
    args, where = [], []
    for k in range(groups):
        array, start = spots[k]
        where.append((len(args), start))
        args.append(array)
    best = call(
        functools.partial(score_blocks_kernel, most, tuple(where)),
        jax.ShapeDtypeStruct((groups, 1, LANES), jnp.float32), args,
    )
    return best, rank, cluster


def exchange_all(embeddings, assignment, most, labels):
    groups = lax.axis_size("clu")
    width = embeddings.shape[1]
    slots = labels * most
    (packed,), _, _, rank, cluster = pack(
        embeddings, assignment, (slots,), most, labels, lambda owner: owner
    )
    arrived = lax.all_to_all(
        packed.reshape(groups, slots // groups, width), "clu",
        split_axis=0, concat_axis=0, tiled=True,
    )
    best = call(
        functools.partial(score_all_kernel, most),
        jax.ShapeDtypeStruct((groups, 1, LANES), jnp.float32), (arrived.reshape(slots, width),),
    )
    return best, rank, cluster


def uses_blocks(groups, most):
    power = groups & (groups - 1) == 0 and groups >= 16
    return power and most % 16 == 0 and LANES % (2 * most) == 0


def shards(embeddings, assignment):
    groups = lax.axis_size("clu")
    count = embeddings.shape[0]
    most = 2 * count // (CLU_DEV * groups)
    labels = CLU_DEV * groups
    relative = uses_blocks(groups, most)
    exchange = exchange_blocks if relative else exchange_all
    best, rank, cluster = exchange(embeddings, assignment, most, labels)
    returned = lax.all_to_all(best, "clu", split_axis=0, concat_axis=0, tiled=True)
    out = call(
        functools.partial(pick_kernel, most, relative),
        jax.ShapeDtypeStruct((1, count), jnp.float32), (returned, rank, cluster),
    )
    return out.reshape(count)


def solution(mesh):
    in_specs = (P(("lang", "clu"), None), P(("lang", "clu"), None))
    out_specs = P(("lang", "clu"))

    return jax.shard_map(shards, mesh=mesh, in_specs=in_specs, out_specs=out_specs, check_vma=False)
```

time: 47 us -> 43.5 us (0.926)
  waiting for transfers between devices: 15.4 us -> 8.36 us
  starting transfers between devices: 17.6 us -> 21.2 us
  blocking collectives: 10.9 us -> 10.4 us
    ppermute x15, waiting for transfers between devices: 15.4 us -> 8.36 us  [swap(): return lax.ppermute(array, 'clu', [(i, i ^ k) for i in range(groups)])]
    ppermute x15, starting transfers between devices: 17.6 us -> 21.2 us  [swap(): return lax.ppermute(array, 'clu', [(i, i ^ k) for i in range(groups)])]
    pallas_call x3 -> x5, Pallas kernels: 2.92 us -> 3.24 us  [call(): pl.pallas_call(kernel, out_shape=out_shape, in_specs=in_specs or [VMEM] *...]
  transfers between devices with their start and end apart: 15 -> 15, of which waited for: 7 -> 4; matrix products, arithmetic and copies ran while one was open for 0% -> 0% of each run, Pallas kernels for 0% -> 2%
where the time goes in v4:
time: 43.5 us; the launch traced here: 43.3 us
  starting transfers between devices  21.2 us (49%)
  blocking collectives  10.4 us (24%)
  waiting for transfers between devices  8.36 us (19%)
  Pallas kernels  3.24 us (7%)
    ppermute x15, starting transfers between devices, swap(): return lax.ppermute(array, 'clu', [(i, i ^ k) for i in range(groups)])  21.2 us
    all_to_all x1, blocking collectives, shards(): lax.all_to_all(best, 'clu', split_axis=0, concat_axis=0, tiled=True)  10.4 us
    ppermute x15, waiting for transfers between devices, swap(): return lax.ppermute(array, 'clu', [(i, i ^ k) for i in range(groups)])  8.36 us
    pallas_call x5, Pallas kernels, call(): pl.pallas_call(kernel, out_shape=out_shape, in_specs=in_specs or [VMEM] *...  3.24 us
  transfers between devices with their start and end apart: 15, of which 4 were waited for; matrix products, arithmetic and copies ran while one was open for 0% of the time, Pallas kernels for 2%

profile of v4, /device:TPU:0, one launch (start us, length us, event | category | flops | bytes accessed | tf_op | source)
XLA Modules:
  0.0 43.3 jit_solution(104106656172906264)
XLA Ops:
  0.0 1.3 %shard_map.28 = (bf16[64,1024]{1,0:T(8,128)(2,1)S(1)}, bf16[64,1024]{1,0:T(8,128)(2,1)S(1)}, bf16[256,1024]{1,0:T(8,128)(2,1)S(1)}, s32[1,256]{1,0:T(1,128)S(1)}...) custom-call(bf16[256,1024]{1,0:T(8,128)(2,1)} %rows_hbm.1, s32[1,256]{1,0:T(1,128)} %bitcast.2), custom_call_target="tpu_custom_call" | custom-call | flops 16777216 | bytes 1048576 | tf_op jit(solution)/shard_map/pallas_call | solution.py:22
  1.3 5.5 %collective-permute-start.11 = (bf16[64,1024]{1,0:T(8,128)(2,1)S(1)}, bf16[64,1024]{1,0:T(8,128)(2,1)S(1)}, u32[]{:S(2)}, u32[]{:S(2)}) collective-permute-start(bf16[64,1024]{1,0:T(8,128)(2,1)S(1)} %get-tuple-element.33), channel_id=1, source_target_pairs={{0,15},{1,14},{2,13},{3,12},{4,11},{5,10},{6,9},{7,8},{8,7},{9,6},... | collective-permute-start | bytes 393224 | tf_op jit(solution)/shard_map/ppermute | solution.py:191
  6.8 0.5 %collective-permute-start.13 = (bf16[64,1024]{1,0:T(8,128)(2,1)S(1)}, bf16[64,1024]{1,0:T(8,128)(2,1)S(1)}, u32[]{:S(2)}, u32[]{:S(2)}) collective-permute-start(bf16[64,1024]{1,0:T(8,128)(2,1)S(1)} %get-tuple-element.34), channel_id=1, source_target_pairs={{0,13},{1,12},{2,15},{3,14},{4,9},{5,8},{6,11},{7,10},{8,5},{9,4},... | collective-permute-start | bytes 393224 | tf_op jit(solution)/shard_map/ppermute | solution.py:191
  7.3 0.5 %shard_map.29 = (bf16[64,1024]{1,0:T(8,128)(2,1)S(1)}, bf16[32,1024]{1,0:T(8,128)(2,1)S(1)}, bf16[64,1024]{1,0:T(8,128)(2,1)S(1)}, bf16[32,1024]{1,0:T(8,128)(2,...) custom-call(bf16[256,1024]{1,0:T(8,128)(2,1)S(1)} %get-tuple-element, ...), custom_call_target="tpu_custom_call" | custom-call | flops 16777216 | bytes 1048576 | tf_op jit(solution)/shard_map/pallas_call | solution.py:22
  7.9 0.5 %collective-permute-start.1 = (bf16[64,1024]{1,0:T(8,128)(2,1)S(1)}, bf16[64,1024]{1,0:T(8,128)(2,1)S(1)}, u32[]{:S(2)}, u32[]{:S(2)}) collective-permute-start(bf16[64,1024]{1,0:T(8,128)(2,1)S(1)} %get-tuple-element.27), channel_id=1, source_target_pairs={{0,3},{1,2},{2,1},{3,0},{4,7},{5,6},{6,5},{7,4},{8,11},{9,10},{10,... | collective-permute-start | bytes 393224 | tf_op jit(solution)/shard_map/ppermute | solution.py:191
  8.4 0.0 collective-permute-start.3
  8.4 2.6 %collective-permute-start.5 = (bf16[64,1024]{1,0:T(8,128)(2,1)S(1)}, bf16[64,1024]{1,0:T(8,128)(2,1)S(1)}, u32[]{:S(2)}, u32[]{:S(2)}) collective-permute-start(bf16[64,1024]{1,0:T(8,128)(2,1)S(1)} %get-tuple-element.29), channel_id=1, source_target_pairs={{0,7},{1,6},{2,5},{3,4},{4,3},{5,2},{6,1},{7,0},{8,15},{9,14},{10,... | collective-permute-start | bytes 393224 | tf_op jit(solution)/shard_map/ppermute | solution.py:191
  10.9 0.0 collective-permute-done.11.refs_0_
  10.9 7.6 %collective-permute-start.9 = (bf16[64,1024]{1,0:T(8,128)(2,1)S(1)}, bf16[64,1024]{1,0:T(8,128)(2,1)S(1)}, u32[]{:S(2)}, u32[]{:S(2)}) collective-permute-start(bf16[64,1024]{1,0:T(8,128)(2,1)S(1)} %get-tuple-element.32), channel_id=1, source_target_pairs={{0,11},{1,10},{2,9},{3,8},{4,15},{5,14},{6,13},{7,12},{8,3},{9,2},... | collective-permute-start | bytes 393224 | tf_op jit(solution)/shard_map/ppermute | solution.py:191
  18.5 0.0 collective-permute-done.13.refs_2_
  18.5 0.7 %collective-permute-start = (bf16[32,1024]{1,0:T(8,128)(2,1)S(1)}, bf16[32,1024]{1,0:T(8,128)(2,1)S(1)}, u32[]{:S(2)}, u32[]{:S(2)}) collective-permute-start(bf16[32,1024]{1,0:T(8,128)(2,1)S(1)} %get-tuple-element.26), channel_id=1, source_target_pairs={{0,1},{1,0},{2,3},{3,2},{4,5},{5,4},{6,7},{7,6},{8,9},{9,8},{10,11... | collective-permute-start | bytes 196616 | tf_op jit(solution)/shard_map/ppermute | solution.py:191
  19.3 0.0 collective-permute-done.1.refs_3_
  19.3 1.5 %collective-permute-start.7 = (bf16[32,1024]{1,0:T(8,128)(2,1)S(1)}, bf16[32,1024]{1,0:T(8,128)(2,1)S(1)}, u32[]{:S(2)}, u32[]{:S(2)}) collective-permute-start(bf16[32,1024]{1,0:T(8,128)(2,1)S(1)} %get-tuple-element.30), channel_id=1, source_target_pairs={{0,8},{1,9},{2,10},{3,11},{4,12},{5,13},{6,14},{7,15},{8,0},{9,1},... | collective-permute-start | bytes 196616 | tf_op jit(solution)/shard_map/ppermute | solution.py:191
  20.8 0.0 collective-permute-done.3.refs_5_
  20.8 0.1 collective-permute-start.12
  20.9 0.3 collective-permute-done.5.refs_7_
  21.2 0.2 collective-permute-start.14
  21.4 4.6 %collective-permute-done.9.refs_11_ = bf16[64,1024]{1,0:T(8,128)(2,1)S(1)} collective-permute-done((bf16[64,1024]{1,0:T(8,128)(2,1)S(1)}, bf16[64,1024]{1,0:T(8,128)(2,1)S(1)}, u32[]{:S(2)}, u32[]{:S(2)}) %collective-permute-start.9) | collective-permute-done | bytes 131104 | tf_op jit(solution)/shard_map/ppermute | solution.py:191
  26.0 0.0 collective-permute-start.8
  26.0 0.0 collective-permute-done.refs_1_
  26.0 1.4 %collective-permute-start.2 = (bf16[32,1024]{1,0:T(8,128)(2,1)S(1)}, bf16[32,1024]{1,0:T(8,128)(2,1)S(1)}, u32[]{:S(2)}, u32[]{:S(2)}) collective-permute-start(bf16[32,1024]{1,0:T(8,128)(2,1)S(1)} %slice.24), channel_id=1, source_target_pairs={{0,1},{1,0},{2,3},{3,2},{4,5},{5,4},{6,7},{7,6},{8,9},{9,8},{10,11... | collective-permute-start | bytes 196616 | tf_op jit(solution)/shard_map/ppermute | solution.py:191
  27.4 0.1 collective-permute-done.7.refs_8_
  27.5 0.0 collective-permute-start.4
  27.5 0.0 collective-permute-done.12.refs_1_
  27.5 0.5 %collective-permute-start.6 = (bf16[32,1024]{1,0:T(8,128)(2,1)S(1)}, bf16[32,1024]{1,0:T(8,128)(2,1)S(1)}, u32[]{:S(2)}, u32[]{:S(2)}) collective-permute-start(bf16[32,1024]{1,0:T(8,128)(2,1)S(1)} %slice.26), channel_id=1, source_target_pairs={{0,1},{1,0},{2,3},{3,2},{4,5},{5,4},{6,7},{7,6},{8,9},{9,8},{10,11... | collective-permute-start | bytes 196616 | tf_op jit(solution)/shard_map/ppermute | solution.py:191
  28.0 0.0 collective-permute-done.14.refs_3_
  28.0 0.1 collective-permute-start.10
  28.1 0.2 shard_map.30
  28.3 3.4 %collective-permute-done.8.refs_9_ = bf16[32,1024]{1,0:T(8,128)(2,1)S(1)} collective-permute-done((bf16[32,1024]{1,0:T(8,128)(2,1)S(1)}, bf16[32,1024]{1,0:T(8,128)(2,1)S(1)}, u32[]{:S(2)}, u32[]{:S(2)}) %collective-permute-start.8) | collective-permute-done | bytes 65568 | tf_op jit(solution)/shard_map/ppermute | solution.py:191
  31.6 0.0 collective-permute-done.2.refs_2_
  31.7 0.0 collective-permute-done.4.refs_4_
  31.7 0.0 collective-permute-done.6.refs_6_
  31.7 0.0 collective-permute-done.10.refs_10_
  31.7 0.6 %shard_map.31 = f32[16,1,128]{2,1,0:T(1,128)S(1)} custom-call(bf16[32,1024]{1,0:T(8,128)(2,1)S(1)} %get-tuple-element.25.refs_0_, bf16[32,1024]{1,0:T(8,128)(2,1)S(1)} %collective-permute-done.refs_1_, bf16[32,1024]{1,0:T(8,128)(2,1)S(1)} %collective-permute-done.2.refs_2_, bf16[64,1024]{1,0:T(8,128)(2,1)S(1)} %collective-permute-done.1.refs_3_, ...), custom_call_target="tpu_custom_call" | custom-call | flops 16777216 | bytes 1048576 | tf_op jit(solution)/shard_map/pallas_call | solution.py:22
  32.2 10.4 %all_to_all.5.best_ref = f32[16,1,128]{2,1,0:T(1,128)S(1)} all-to-all(f32[16,1,128]{2,1,0:T(1,128)S(1)} %shard_map.31), channel_id=1, replica_groups=mesh['lang'=2,'clu'=16] {'clu'}, dimensions={0} | all-to-all | bytes 16384 | tf_op jit(solution)/shard_map/all_to_all | solution.py:284
  42.7 0.7 %shard_map.32 = f32[1,256]{1,0:T(1,128)} custom-call(f32[16,1,128]{2,1,0:T(1,128)S(1)} %all_to_all.5.best_ref, s32[1,256]{1,0:T(1,128)S(1)} %get-tuple-element.39.rank_ref, s32[1,256]{1,0:T(1,128)S(1)} %get-tuple-element.40.cluster_ref), custom_call_target="tpu_custom_call" | custom-call | flops 16777216 | bytes 1048576 | tf_op jit(solution)/shard_map/pallas_call | solution.py:22
  (6 shorter events, 0.0 us)
Async XLA Ops:
  1.3 9.6 %collective-permute-start.11 = (bf16[64,1024]{1,0:T(8,128)(2,1)S(1)}, bf16[64,1024]{1,0:T(8,128)(2,1)S(1)}, u32[]{:S(2)}, u32[]{:S(2)}) collective-permute-start(bf16[64,1024]{1,0:T(8,128)(2,1)S(1)} %get-tuple-element.33), channel_id=1, source_target_pairs={{0,15},{1,14},{2,13},{3,12},{4,11},{5,10},{6,9},{7,8},{8,7},{9,6},... | collective-permute-start | bytes 393224 | tf_op jit(solution)/shard_map/ppermute | solution.py:191
  6.8 11.7 %collective-permute-start.13 = (bf16[64,1024]{1,0:T(8,128)(2,1)S(1)}, bf16[64,1024]{1,0:T(8,128)(2,1)S(1)}, u32[]{:S(2)}, u32[]{:S(2)}) collective-permute-start(bf16[64,1024]{1,0:T(8,128)(2,1)S(1)} %get-tuple-element.34), channel_id=1, source_target_pairs={{0,13},{1,12},{2,15},{3,14},{4,9},{5,8},{6,11},{7,10},{8,5},{9,4},... | collective-permute-start | bytes 393224 | tf_op jit(solution)/shard_map/ppermute | solution.py:191
  7.9 11.4 %collective-permute-start.1 = (bf16[64,1024]{1,0:T(8,128)(2,1)S(1)}, bf16[64,1024]{1,0:T(8,128)(2,1)S(1)}, u32[]{:S(2)}, u32[]{:S(2)}) collective-permute-start(bf16[64,1024]{1,0:T(8,128)(2,1)S(1)} %get-tuple-element.27), channel_id=1, source_target_pairs={{0,3},{1,2},{2,1},{3,0},{4,7},{5,6},{6,5},{7,4},{8,11},{9,10},{10,... | collective-permute-start | bytes 393224 | tf_op jit(solution)/shard_map/ppermute | solution.py:191
  8.4 12.4 %collective-permute-start.3 = (bf16[64,1024]{1,0:T(8,128)(2,1)S(1)}, bf16[64,1024]{1,0:T(8,128)(2,1)S(1)}, u32[]{:S(2)}, u32[]{:S(2)}) collective-permute-start(bf16[64,1024]{1,0:T(8,128)(2,1)S(1)} %get-tuple-element.28), channel_id=1, source_target_pairs={{0,5},{1,4},{2,7},{3,6},{4,1},{5,0},{6,3},{7,2},{8,13},{9,12},{10,... | collective-permute-start | bytes 393224 | tf_op jit(solution)/shard_map/ppermute | solution.py:191
  8.4 12.8 %collective-permute-start.5 = (bf16[64,1024]{1,0:T(8,128)(2,1)S(1)}, bf16[64,1024]{1,0:T(8,128)(2,1)S(1)}, u32[]{:S(2)}, u32[]{:S(2)}) collective-permute-start(bf16[64,1024]{1,0:T(8,128)(2,1)S(1)} %get-tuple-element.29), channel_id=1, source_target_pairs={{0,7},{1,6},{2,5},{3,4},{4,3},{5,2},{6,1},{7,0},{8,15},{9,14},{10,... | collective-permute-start | bytes 393224 | tf_op jit(solution)/shard_map/ppermute | solution.py:191
  10.9 15.0 %collective-permute-start.9 = (bf16[64,1024]{1,0:T(8,128)(2,1)S(1)}, bf16[64,1024]{1,0:T(8,128)(2,1)S(1)}, u32[]{:S(2)}, u32[]{:S(2)}) collective-permute-start(bf16[64,1024]{1,0:T(8,128)(2,1)S(1)} %get-tuple-element.32), channel_id=1, source_target_pairs={{0,11},{1,10},{2,9},{3,8},{4,15},{5,14},{6,13},{7,12},{8,3},{9,2},... | collective-permute-start | bytes 393224 | tf_op jit(solution)/shard_map/ppermute | solution.py:191
  18.5 7.5 %collective-permute-start = (bf16[32,1024]{1,0:T(8,128)(2,1)S(1)}, bf16[32,1024]{1,0:T(8,128)(2,1)S(1)}, u32[]{:S(2)}, u32[]{:S(2)}) collective-permute-start(bf16[32,1024]{1,0:T(8,128)(2,1)S(1)} %get-tuple-element.26), channel_id=1, source_target_pairs={{0,1},{1,0},{2,3},{3,2},{4,5},{5,4},{6,7},{7,6},{8,9},{9,8},{10,11... | collective-permute-start | bytes 196616 | tf_op jit(solution)/shard_map/ppermute | solution.py:191
  19.3 8.3 %collective-permute-start.7 = (bf16[32,1024]{1,0:T(8,128)(2,1)S(1)}, bf16[32,1024]{1,0:T(8,128)(2,1)S(1)}, u32[]{:S(2)}, u32[]{:S(2)}) collective-permute-start(bf16[32,1024]{1,0:T(8,128)(2,1)S(1)} %get-tuple-element.30), channel_id=1, source_target_pairs={{0,8},{1,9},{2,10},{3,11},{4,12},{5,13},{6,14},{7,15},{8,0},{9,1},... | collective-permute-start | bytes 196616 | tf_op jit(solution)/shard_map/ppermute | solution.py:191
  20.8 6.7 %collective-permute-start.12 = (bf16[32,1024]{1,0:T(8,128)(2,1)S(1)}, bf16[32,1024]{1,0:T(8,128)(2,1)S(1)}, u32[]{:S(2)}, u32[]{:S(2)}) collective-permute-start(bf16[32,1024]{1,0:T(8,128)(2,1)S(1)} %slice.28), channel_id=1, source_target_pairs={{0,1},{1,0},{2,3},{3,2},{4,5},{5,4},{6,7},{7,6},{8,9},{9,8},{10,11... | collective-permute-start | bytes 196616 | tf_op jit(solution)/shard_map/ppermute | solution.py:191
  21.2 6.8 %collective-permute-start.14 = (bf16[32,1024]{1,0:T(8,128)(2,1)S(1)}, bf16[32,1024]{1,0:T(8,128)(2,1)S(1)}, u32[]{:S(2)}, u32[]{:S(2)}) collective-permute-start(bf16[32,1024]{1,0:T(8,128)(2,1)S(1)} %slice.29), channel_id=1, source_target_pairs={{0,1},{1,0},{2,3},{3,2},{4,5},{5,4},{6,7},{7,6},{8,9},{9,8},{10,11... | collective-permute-start | bytes 196616 | tf_op jit(solution)/shard_map/ppermute | solution.py:191
  26.0 5.7 %collective-permute-start.8 = (bf16[32,1024]{1,0:T(8,128)(2,1)S(1)}, bf16[32,1024]{1,0:T(8,128)(2,1)S(1)}, u32[]{:S(2)}, u32[]{:S(2)}) collective-permute-start(bf16[32,1024]{1,0:T(8,128)(2,1)S(1)} %get-tuple-element.31), channel_id=1, source_target_pairs={{0,9},{1,8},{2,11},{3,10},{4,13},{5,12},{6,15},{7,14},{8,1},{9,0},... | collective-permute-start | bytes 196616 | tf_op jit(solution)/shard_map/ppermute | solution.py:191
  26.0 5.7 %collective-permute-start.2 = (bf16[32,1024]{1,0:T(8,128)(2,1)S(1)}, bf16[32,1024]{1,0:T(8,128)(2,1)S(1)}, u32[]{:S(2)}, u32[]{:S(2)}) collective-permute-start(bf16[32,1024]{1,0:T(8,128)(2,1)S(1)} %slice.24), channel_id=1, source_target_pairs={{0,1},{1,0},{2,3},{3,2},{4,5},{5,4},{6,7},{7,6},{8,9},{9,8},{10,11... | collective-permute-start | bytes 196616 | tf_op jit(solution)/shard_map/ppermute | solution.py:191
  27.5 4.1 %collective-permute-start.4 = (bf16[32,1024]{1,0:T(8,128)(2,1)S(1)}, bf16[32,1024]{1,0:T(8,128)(2,1)S(1)}, u32[]{:S(2)}, u32[]{:S(2)}) collective-permute-start(bf16[32,1024]{1,0:T(8,128)(2,1)S(1)} %slice.25), channel_id=1, source_target_pairs={{0,1},{1,0},{2,3},{3,2},{4,5},{5,4},{6,7},{7,6},{8,9},{9,8},{10,11... | collective-permute-start | bytes 196616 | tf_op jit(solution)/shard_map/ppermute | solution.py:191
  27.5 4.1 %collective-permute-start.6 = (bf16[32,1024]{1,0:T(8,128)(2,1)S(1)}, bf16[32,1024]{1,0:T(8,128)(2,1)S(1)}, u32[]{:S(2)}, u32[]{:S(2)}) collective-permute-start(bf16[32,1024]{1,0:T(8,128)(2,1)S(1)} %slice.26), channel_id=1, source_target_pairs={{0,1},{1,0},{2,3},{3,2},{4,5},{5,4},{6,7},{7,6},{8,9},{9,8},{10,11... | collective-permute-start | bytes 196616 | tf_op jit(solution)/shard_map/ppermute | solution.py:191
  28.0 3.6 %collective-permute-start.10 = (bf16[32,1024]{1,0:T(8,128)(2,1)S(1)}, bf16[32,1024]{1,0:T(8,128)(2,1)S(1)}, u32[]{:S(2)}, u32[]{:S(2)}) collective-permute-start(bf16[32,1024]{1,0:T(8,128)(2,1)S(1)} %slice.27), channel_id=1, source_target_pairs={{0,1},{1,0},{2,3},{3,2},{4,5},{5,4},{6,7},{7,6},{8,9},{9,8},{10,11... | collective-permute-start | bytes 196616 | tf_op jit(solution)/shard_map/ppermute | solution.py:191

commit v5 on v4

--- a/solution.py
+++ b/solution.py
@@ -193,17 +193,17 @@
 
 def message_order(groups):
     chips = groups // 2
-    last = chips // 2
-    far = [2 * m + 1 for m in range(chips - 1, last - 1, -1)]
-    near = [2 * m + 1 for m in range(last - 1, 0, -1)]
-    return [*far, near[-1], 2 * last, *near[:-1], 1]
+    last = groups - 2
+    far = [2 * m + 1 for m in range(chips - 2, chips // 2 - 1, -1)]
+    near = [2 * m + 1 for m in range(2, chips // 2)]
+    return [*far, *near, last + 1, 3, last, 1]
 
 
 def exchange_blocks(embeddings, assignment, most, labels):
     groups = lax.axis_size("clu")
     width = embeddings.shape[1]
     block = CLU_DEV * most
-    last = groups // 2
+    last = groups - 2
     order = message_order(groups)
     held = [[k] if k in (last, last + 1, 1) else [k, k - 1] for k in order] + [[0]]
     flat = [k for blocks in held for k in blocks]
@@ -216,7 +216,7 @@
             spot = jnp.where(k == value, n, spot)
         return spot
 
-    ahead = 2
+    ahead = 1
     packed, rows, position, rank, cluster = pack(
         embeddings, assignment, tuple(sizes[:ahead]), most, labels, block_of
     )

time: 43.5 us -> 43.2 us (level)
  starting transfers between devices: 21.2 us -> 20 us
  waiting for transfers between devices: 8.36 us -> 9.18 us
    ppermute x15, starting transfers between devices: 21.2 us -> 20 us  [swap(): return lax.ppermute(array, 'clu', [(i, i ^ k) for i in range(groups)])]
    ppermute x15, waiting for transfers between devices: 8.36 us -> 9.18 us  [swap(): return lax.ppermute(array, 'clu', [(i, i ^ k) for i in range(groups)])]
  transfers between devices with their start and end apart: 15 -> 15, of which waited for: 4 -> 7; matrix products, arithmetic and copies ran while one was open for 0% -> 0% of each run, Pallas kernels for 2% -> 2%
where the time goes in v5:
time: 43.2 us; the launch traced here: 43 us
  starting transfers between devices  20 us (46%)
  blocking collectives  10.5 us (24%)
  waiting for transfers between devices  9.18 us (21%)
  Pallas kernels  3.22 us (7%)
    ppermute x15, starting transfers between devices, swap(): return lax.ppermute(array, 'clu', [(i, i ^ k) for i in range(groups)])  20 us
    all_to_all x1, blocking collectives, shards(): lax.all_to_all(best, 'clu', split_axis=0, concat_axis=0, tiled=True)  10.5 us
    ppermute x15, waiting for transfers between devices, swap(): return lax.ppermute(array, 'clu', [(i, i ^ k) for i in range(groups)])  9.18 us
    pallas_call x5, Pallas kernels, call(): pl.pallas_call(kernel, out_shape=out_shape, in_specs=in_specs or [VMEM] *...  3.22 us
  transfers between devices with their start and end apart: 15, of which 7 were waited for; matrix products, arithmetic and copies ran while one was open for 0% of the time, Pallas kernels for 2%

profile of v5, /device:TPU:0, one launch (start us, length us, event | category | flops | bytes accessed | tf_op | source)
XLA Modules:
  0.0 43.0 jit_solution(9116227809560075860)
XLA Ops:
  0.0 1.3 %shard_map.28 = (bf16[64,1024]{1,0:T(8,128)(2,1)S(1)}, bf16[256,1024]{1,0:T(8,128)(2,1)S(1)}, s32[1,256]{1,0:T(1,128)S(1)}, s32[1,256]{1,0:T(1,128)S(1)}, s32[1,256]{1,0:T(1,128)S(1)}) custom-call(bf16[256,1024]{1,0:T(8,128)(2,1)} %rows_hbm.1, s32[1,256]{1,0:T(1,128)} %bitcast.2), custom_call_target="tpu_custom_call" | custom-call | flops 16777216 | bytes 1048576 | tf_op jit(solution)/shard_map/pallas_call | solution.py:22
  1.3 4.6 %collective-permute-start.11 = (bf16[64,1024]{1,0:T(8,128)(2,1)S(1)}, bf16[64,1024]{1,0:T(8,128)(2,1)S(1)}, u32[]{:S(2)}, u32[]{:S(2)}) collective-permute-start(bf16[64,1024]{1,0:T(8,128)(2,1)S(1)} %get-tuple-element.30), channel_id=1, source_target_pairs={{0,13},{1,12},{2,15},{3,14},{4,9},{5,8},{6,11},{7,10},{8,5},{9,4},... | collective-permute-start | bytes 393224 | tf_op jit(solution)/shard_map/ppermute | solution.py:191
  5.9 0.6 %shard_map.29 = (bf16[64,1024]{1,0:T(8,128)(2,1)S(1)}, bf16[64,1024]{1,0:T(8,128)(2,1)S(1)}, bf16[64,1024]{1,0:T(8,128)(2,1)S(1)}, bf16[64,1024]{1,0:T(8,128)(2,...) custom-call(bf16[256,1024]{1,0:T(8,128)(2,1)S(1)} %get-tuple-element, ...), custom_call_target="tpu_custom_call" | custom-call | flops 16777216 | bytes 1048576 | tf_op jit(solution)/shard_map/pallas_call | solution.py:22
  6.5 1.8 %collective-permute-start.1 = (bf16[64,1024]{1,0:T(8,128)(2,1)S(1)}, bf16[64,1024]{1,0:T(8,128)(2,1)S(1)}, u32[]{:S(2)}, u32[]{:S(2)}) collective-permute-start(bf16[64,1024]{1,0:T(8,128)(2,1)S(1)} %get-tuple-element.25), channel_id=1, source_target_pairs={{0,3},{1,2},{2,1},{3,0},{4,7},{5,6},{6,5},{7,4},{8,11},{9,10},{10,... | collective-permute-start | bytes 393224 | tf_op jit(solution)/shard_map/ppermute | solution.py:191
  8.3 0.0 collective-permute-start.3
  8.3 1.7 %collective-permute-start.5 = (bf16[64,1024]{1,0:T(8,128)(2,1)S(1)}, bf16[64,1024]{1,0:T(8,128)(2,1)S(1)}, u32[]{:S(2)}, u32[]{:S(2)}) collective-permute-start(bf16[64,1024]{1,0:T(8,128)(2,1)S(1)} %get-tuple-element.27), channel_id=1, source_target_pairs={{0,7},{1,6},{2,5},{3,4},{4,3},{5,2},{6,1},{7,0},{8,15},{9,14},{10,... | collective-permute-start | bytes 393224 | tf_op jit(solution)/shard_map/ppermute | solution.py:191
  10.0 0.0 collective-permute-start.7
  10.0 0.0 collective-permute-done.11.refs_0_
  10.0 4.7 %collective-permute-start.9 = (bf16[64,1024]{1,0:T(8,128)(2,1)S(1)}, bf16[64,1024]{1,0:T(8,128)(2,1)S(1)}, u32[]{:S(2)}, u32[]{:S(2)}) collective-permute-start(bf16[64,1024]{1,0:T(8,128)(2,1)S(1)} %get-tuple-element.29), channel_id=1, source_target_pairs={{0,11},{1,10},{2,9},{3,8},{4,15},{5,14},{6,13},{7,12},{8,3},{9,2},... | collective-permute-start | bytes 393224 | tf_op jit(solution)/shard_map/ppermute | solution.py:191
  14.7 0.0 collective-permute-done.1.refs_3_
  14.7 0.4 %collective-permute-start = (bf16[32,1024]{1,0:T(8,128)(2,1)S(1)}, bf16[32,1024]{1,0:T(8,128)(2,1)S(1)}, u32[]{:S(2)}, u32[]{:S(2)}) collective-permute-start(bf16[32,1024]{1,0:T(8,128)(2,1)S(1)} %get-tuple-element.24), channel_id=1, source_target_pairs={{0,1},{1,0},{2,3},{3,2},{4,5},{5,4},{6,7},{7,6},{8,9},{9,8},{10,11... | collective-permute-start | bytes 196616 | tf_op jit(solution)/shard_map/ppermute | solution.py:191
  15.2 0.8 %collective-permute-done.3.refs_5_ = bf16[64,1024]{1,0:T(8,128)(2,1)S(1)} collective-permute-done((bf16[64,1024]{1,0:T(8,128)(2,1)S(1)}, bf16[64,1024]{1,0:T(8,128)(2,1)S(1)}, u32[]{:S(2)}, u32[]{:S(2)}) %collective-permute-start.3) | collective-permute-done | bytes 131104 | tf_op jit(solution)/shard_map/ppermute | solution.py:191
  15.9 0.4 %collective-permute-start.13 = (bf16[32,1024]{1,0:T(8,128)(2,1)S(1)}, bf16[32,1024]{1,0:T(8,128)(2,1)S(1)}, u32[]{:S(2)}, u32[]{:S(2)}) collective-permute-start(bf16[32,1024]{1,0:T(8,128)(2,1)S(1)} %get-tuple-element.33), channel_id=1, source_target_pairs={{0,14},{1,15},{2,12},{3,13},{4,10},{5,11},{6,8},{7,9},{8,6},{9,7},... | collective-permute-start | bytes 196616 | tf_op jit(solution)/shard_map/ppermute | solution.py:191
  16.4 3.0 %collective-permute-done.5.refs_7_ = bf16[64,1024]{1,0:T(8,128)(2,1)S(1)} collective-permute-done((bf16[64,1024]{1,0:T(8,128)(2,1)S(1)}, bf16[64,1024]{1,0:T(8,128)(2,1)S(1)}, u32[]{:S(2)}, u32[]{:S(2)}) %collective-permute-start.5) | collective-permute-done | bytes 131104 | tf_op jit(solution)/shard_map/ppermute | solution.py:191
  19.3 4.8 %collective-permute-start.14 = (bf16[32,1024]{1,0:T(8,128)(2,1)S(1)}, bf16[32,1024]{1,0:T(8,128)(2,1)S(1)}, u32[]{:S(2)}, u32[]{:S(2)}) collective-permute-start(bf16[32,1024]{1,0:T(8,128)(2,1)S(1)} %get-tuple-element.34), channel_id=1, source_target_pairs={{0,15},{1,14},{2,13},{3,12},{4,11},{5,10},{6,9},{7,8},{8,7},{9,6},... | collective-permute-start | bytes 196616 | tf_op jit(solution)/shard_map/ppermute | solution.py:191
  24.1 0.0 collective-permute-done.7.refs_9_
  24.1 0.4 collective-permute-start.12
  24.5 4.4 %collective-permute-done.9.refs_11_ = bf16[64,1024]{1,0:T(8,128)(2,1)S(1)} collective-permute-done((bf16[64,1024]{1,0:T(8,128)(2,1)S(1)}, bf16[64,1024]{1,0:T(8,128)(2,1)S(1)}, u32[]{:S(2)}, u32[]{:S(2)}) %collective-permute-start.9) | collective-permute-done | bytes 131104 | tf_op jit(solution)/shard_map/ppermute | solution.py:191
  28.9 0.1 collective-permute-start.2
  29.1 0.0 collective-permute-done.refs_1_
  29.1 0.5 %collective-permute-start.4 = (bf16[32,1024]{1,0:T(8,128)(2,1)S(1)}, bf16[32,1024]{1,0:T(8,128)(2,1)S(1)}, u32[]{:S(2)}, u32[]{:S(2)}) collective-permute-start(bf16[32,1024]{1,0:T(8,128)(2,1)S(1)} %slice.25), channel_id=1, source_target_pairs={{0,1},{1,0},{2,3},{3,2},{4,5},{5,4},{6,7},{7,6},{8,9},{9,8},{10,11... | collective-permute-start | bytes 196616 | tf_op jit(solution)/shard_map/ppermute | solution.py:191
  29.5 0.0 collective-permute-done.13.refs_14_
  29.5 0.1 collective-permute-start.6
  29.6 0.0 collective-permute-done.14.refs_15_
  29.6 0.4 collective-permute-start.8
  30.0 0.0 collective-permute-done.12.refs_1_
  30.0 0.1 collective-permute-start.10
  30.2 0.1 shard_map.30
  30.3 0.0 collective-permute-done.2.refs_2_
  30.3 0.1 collective-permute-done.4.refs_4_
  30.4 0.4 collective-permute-done.6.refs_6_
  30.8 0.2 collective-permute-done.8.refs_8_
  30.9 0.4 collective-permute-done.10.refs_10_
  31.3 0.6 %shard_map.31 = f32[16,1,128]{2,1,0:T(1,128)S(1)} custom-call(bf16[32,1024]{1,0:T(8,128)(2,1)S(1)} %get-tuple-element.23.refs_0_, bf16[32,1024]{1,0:T(8,128)(2,1)S(1)} %collective-permute-done.refs_1_, bf16[32,1024]{1,0:T(8,128)(2,1)S(1)} %collective-permute-done.2.refs_2_, bf16[64,1024]{1,0:T(8,128)(2,1)S(1)} %collective-permute-done.1.refs_3_, ...), custom_call_target="tpu_custom_call" | custom-call | flops 16777216 | bytes 1048576 | tf_op jit(solution)/shard_map/pallas_call | solution.py:22
  31.9 10.5 %all_to_all.5.best_ref = f32[16,1,128]{2,1,0:T(1,128)S(1)} all-to-all(f32[16,1,128]{2,1,0:T(1,128)S(1)} %shard_map.31), channel_id=1, replica_groups=mesh['lang'=2,'clu'=16] {'clu'}, dimensions={0} | all-to-all | bytes 16384 | tf_op jit(solution)/shard_map/all_to_all | solution.py:284
  42.4 0.7 %shard_map.32 = f32[1,256]{1,0:T(1,128)} custom-call(f32[16,1,128]{2,1,0:T(1,128)S(1)} %all_to_all.5.best_ref, s32[1,256]{1,0:T(1,128)S(1)} %get-tuple-element.35.rank_ref, s32[1,256]{1,0:T(1,128)S(1)} %get-tuple-element.36.cluster_ref), custom_call_target="tpu_custom_call" | custom-call | flops 16777216 | bytes 1048576 | tf_op jit(solution)/shard_map/pallas_call | solution.py:22
  (6 shorter events, 0.0 us)
Async XLA Ops:
  1.3 8.7 %collective-permute-start.11 = (bf16[64,1024]{1,0:T(8,128)(2,1)S(1)}, bf16[64,1024]{1,0:T(8,128)(2,1)S(1)}, u32[]{:S(2)}, u32[]{:S(2)}) collective-permute-start(bf16[64,1024]{1,0:T(8,128)(2,1)S(1)} %get-tuple-element.30), channel_id=1, source_target_pairs={{0,13},{1,12},{2,15},{3,14},{4,9},{5,8},{6,11},{7,10},{8,5},{9,4},... | collective-permute-start | bytes 393224 | tf_op jit(solution)/shard_map/ppermute | solution.py:191
  6.5 8.2 %collective-permute-start.1 = (bf16[64,1024]{1,0:T(8,128)(2,1)S(1)}, bf16[64,1024]{1,0:T(8,128)(2,1)S(1)}, u32[]{:S(2)}, u32[]{:S(2)}) collective-permute-start(bf16[64,1024]{1,0:T(8,128)(2,1)S(1)} %get-tuple-element.25), channel_id=1, source_target_pairs={{0,3},{1,2},{2,1},{3,0},{4,7},{5,6},{6,5},{7,4},{8,11},{9,10},{10,... | collective-permute-start | bytes 393224 | tf_op jit(solution)/shard_map/ppermute | solution.py:191
  8.3 7.6 %collective-permute-start.3 = (bf16[64,1024]{1,0:T(8,128)(2,1)S(1)}, bf16[64,1024]{1,0:T(8,128)(2,1)S(1)}, u32[]{:S(2)}, u32[]{:S(2)}) collective-permute-start(bf16[64,1024]{1,0:T(8,128)(2,1)S(1)} %get-tuple-element.26), channel_id=1, source_target_pairs={{0,5},{1,4},{2,7},{3,6},{4,1},{5,0},{6,3},{7,2},{8,13},{9,12},{10,... | collective-permute-start | bytes 393224 | tf_op jit(solution)/shard_map/ppermute | solution.py:191
  8.3 11.0 %collective-permute-start.5 = (bf16[64,1024]{1,0:T(8,128)(2,1)S(1)}, bf16[64,1024]{1,0:T(8,128)(2,1)S(1)}, u32[]{:S(2)}, u32[]{:S(2)}) collective-permute-start(bf16[64,1024]{1,0:T(8,128)(2,1)S(1)} %get-tuple-element.27), channel_id=1, source_target_pairs={{0,7},{1,6},{2,5},{3,4},{4,3},{5,2},{6,1},{7,0},{8,15},{9,14},{10,... | collective-permute-start | bytes 393224 | tf_op jit(solution)/shard_map/ppermute | solution.py:191
  10.0 14.1 %collective-permute-start.7 = (bf16[64,1024]{1,0:T(8,128)(2,1)S(1)}, bf16[64,1024]{1,0:T(8,128)(2,1)S(1)}, u32[]{:S(2)}, u32[]{:S(2)}) collective-permute-start(bf16[64,1024]{1,0:T(8,128)(2,1)S(1)} %get-tuple-element.28), channel_id=1, source_target_pairs={{0,9},{1,8},{2,11},{3,10},{4,13},{5,12},{6,15},{7,14},{8,1},{9,0},... | collective-permute-start | bytes 393224 | tf_op jit(solution)/shard_map/ppermute | solution.py:191
  10.0 18.9 %collective-permute-start.9 = (bf16[64,1024]{1,0:T(8,128)(2,1)S(1)}, bf16[64,1024]{1,0:T(8,128)(2,1)S(1)}, u32[]{:S(2)}, u32[]{:S(2)}) collective-permute-start(bf16[64,1024]{1,0:T(8,128)(2,1)S(1)} %get-tuple-element.29), channel_id=1, source_target_pairs={{0,11},{1,10},{2,9},{3,8},{4,15},{5,14},{6,13},{7,12},{8,3},{9,2},... | collective-permute-start | bytes 393224 | tf_op jit(solution)/shard_map/ppermute | solution.py:191
  14.7 14.3 %collective-permute-start = (bf16[32,1024]{1,0:T(8,128)(2,1)S(1)}, bf16[32,1024]{1,0:T(8,128)(2,1)S(1)}, u32[]{:S(2)}, u32[]{:S(2)}) collective-permute-start(bf16[32,1024]{1,0:T(8,128)(2,1)S(1)} %get-tuple-element.24), channel_id=1, source_target_pairs={{0,1},{1,0},{2,3},{3,2},{4,5},{5,4},{6,7},{7,6},{8,9},{9,8},{10,11... | collective-permute-start | bytes 196616 | tf_op jit(solution)/shard_map/ppermute | solution.py:191
  15.9 13.6 %collective-permute-start.13 = (bf16[32,1024]{1,0:T(8,128)(2,1)S(1)}, bf16[32,1024]{1,0:T(8,128)(2,1)S(1)}, u32[]{:S(2)}, u32[]{:S(2)}) collective-permute-start(bf16[32,1024]{1,0:T(8,128)(2,1)S(1)} %get-tuple-element.33), channel_id=1, source_target_pairs={{0,14},{1,15},{2,12},{3,13},{4,10},{5,11},{6,8},{7,9},{8,6},{9,7},... | collective-permute-start | bytes 196616 | tf_op jit(solution)/shard_map/ppermute | solution.py:191
  19.3 10.3 %collective-permute-start.14 = (bf16[32,1024]{1,0:T(8,128)(2,1)S(1)}, bf16[32,1024]{1,0:T(8,128)(2,1)S(1)}, u32[]{:S(2)}, u32[]{:S(2)}) collective-permute-start(bf16[32,1024]{1,0:T(8,128)(2,1)S(1)} %get-tuple-element.34), channel_id=1, source_target_pairs={{0,15},{1,14},{2,13},{3,12},{4,11},{5,10},{6,9},{7,8},{8,7},{9,6},... | collective-permute-start | bytes 196616 | tf_op jit(solution)/shard_map/ppermute | solution.py:191
  24.1 5.9 %collective-permute-start.12 = (bf16[32,1024]{1,0:T(8,128)(2,1)S(1)}, bf16[32,1024]{1,0:T(8,128)(2,1)S(1)}, u32[]{:S(2)}, u32[]{:S(2)}) collective-permute-start(bf16[32,1024]{1,0:T(8,128)(2,1)S(1)} %slice.29), channel_id=1, source_target_pairs={{0,1},{1,0},{2,3},{3,2},{4,5},{5,4},{6,7},{7,6},{8,9},{9,8},{10,11... | collective-permute-start | bytes 196616 | tf_op jit(solution)/shard_map/ppermute | solution.py:191
  28.9 1.4 %collective-permute-start.2 = (bf16[32,1024]{1,0:T(8,128)(2,1)S(1)}, bf16[32,1024]{1,0:T(8,128)(2,1)S(1)}, u32[]{:S(2)}, u32[]{:S(2)}) collective-permute-start(bf16[32,1024]{1,0:T(8,128)(2,1)S(1)} %slice.24), channel_id=1, source_target_pairs={{0,1},{1,0},{2,3},{3,2},{4,5},{5,4},{6,7},{7,6},{8,9},{9,8},{10,11... | collective-permute-start | bytes 196616 | tf_op jit(solution)/shard_map/ppermute | solution.py:191
  29.1 1.4 %collective-permute-start.4 = (bf16[32,1024]{1,0:T(8,128)(2,1)S(1)}, bf16[32,1024]{1,0:T(8,128)(2,1)S(1)}, u32[]{:S(2)}, u32[]{:S(2)}) collective-permute-start(bf16[32,1024]{1,0:T(8,128)(2,1)S(1)} %slice.25), channel_id=1, source_target_pairs={{0,1},{1,0},{2,3},{3,2},{4,5},{5,4},{6,7},{7,6},{8,9},{9,8},{10,11... | collective-permute-start | bytes 196616 | tf_op jit(solution)/shard_map/ppermute | solution.py:191
  29.5 1.3 %collective-permute-start.6 = (bf16[32,1024]{1,0:T(8,128)(2,1)S(1)}, bf16[32,1024]{1,0:T(8,128)(2,1)S(1)}, u32[]{:S(2)}, u32[]{:S(2)}) collective-permute-start(bf16[32,1024]{1,0:T(8,128)(2,1)S(1)} %slice.26), channel_id=1, source_target_pairs={{0,1},{1,0},{2,3},{3,2},{4,5},{5,4},{6,7},{7,6},{8,9},{9,8},{10,11... | collective-permute-start | bytes 196616 | tf_op jit(solution)/shard_map/ppermute | solution.py:191
  29.6 1.3 %collective-permute-start.8 = (bf16[32,1024]{1,0:T(8,128)(2,1)S(1)}, bf16[32,1024]{1,0:T(8,128)(2,1)S(1)}, u32[]{:S(2)}, u32[]{:S(2)}) collective-permute-start(bf16[32,1024]{1,0:T(8,128)(2,1)S(1)} %slice.27), channel_id=1, source_target_pairs={{0,1},{1,0},{2,3},{3,2},{4,5},{5,4},{6,7},{7,6},{8,9},{9,8},{10,11... | collective-permute-start | bytes 196616 | tf_op jit(solution)/shard_map/ppermute | solution.py:191
  30.0 1.3 %collective-permute-start.10 = (bf16[32,1024]{1,0:T(8,128)(2,1)S(1)}, bf16[32,1024]{1,0:T(8,128)(2,1)S(1)}, u32[]{:S(2)}, u32[]{:S(2)}) collective-permute-start(bf16[32,1024]{1,0:T(8,128)(2,1)S(1)} %slice.28), channel_id=1, source_target_pairs={{0,1},{1,0},{2,3},{3,2},{4,5},{5,4},{6,7},{7,6},{8,9},{9,8},{10,11... | collective-permute-start | bytes 196616 | tf_op jit(solution)/shard_map/ppermute | solution.py:191

commit v6 on v5

--- a/solution.py
+++ b/solution.py
@@ -193,17 +193,17 @@
 
 def message_order(groups):
     chips = groups // 2
-    last = groups - 2
-    far = [2 * m + 1 for m in range(chips - 2, chips // 2 - 1, -1)]
-    near = [2 * m + 1 for m in range(2, chips // 2)]
-    return [*far, *near, last + 1, 3, last, 1]
+    last = groups - 4
+    far = [2 * m + 1 for m in (chips - 1, *range(chips - 3, chips // 2 - 1, -1))]
+    near = [2 * m + 1 for m in range(chips // 2 - 1, 0, -1)]
+    return [*far, *near, last + 1, last, 1]
 
 
 def exchange_blocks(embeddings, assignment, most, labels):
     groups = lax.axis_size("clu")
     width = embeddings.shape[1]
     block = CLU_DEV * most
-    last = groups - 2
+    last = groups - 4
     order = message_order(groups)
     held = [[k] if k in (last, last + 1, 1) else [k, k - 1] for k in order] + [[0]]
     flat = [k for blocks in held for k in blocks]

time: 43.2 us -> 43.3 us (level)
  waiting for transfers between devices: 9.18 us -> 8.34 us
  starting transfers between devices: 20 us -> 20.7 us
    ppermute x15, waiting for transfers between devices: 9.18 us -> 8.34 us  [swap(): return lax.ppermute(array, 'clu', [(i, i ^ k) for i in range(groups)])]
    ppermute x15, starting transfers between devices: 20 us -> 20.7 us  [swap(): return lax.ppermute(array, 'clu', [(i, i ^ k) for i in range(groups)])]
where the time goes in v6:
time: 43.3 us; the launch traced here: 43.2 us
  starting transfers between devices  20.7 us (48%)
  blocking collectives  10.8 us (25%)
  waiting for transfers between devices  8.34 us (19%)
  Pallas kernels  3.22 us (7%)
    ppermute x15, starting transfers between devices, swap(): return lax.ppermute(array, 'clu', [(i, i ^ k) for i in range(groups)])  20.7 us
    all_to_all x1, blocking collectives, shards(): lax.all_to_all(best, 'clu', split_axis=0, concat_axis=0, tiled=True)  10.8 us
    ppermute x15, waiting for transfers between devices, swap(): return lax.ppermute(array, 'clu', [(i, i ^ k) for i in range(groups)])  8.34 us
    pallas_call x5, Pallas kernels, call(): pl.pallas_call(kernel, out_shape=out_shape, in_specs=in_specs or [VMEM] *...  3.22 us
  transfers between devices with their start and end apart: 15, of which 7 were waited for; matrix products, arithmetic and copies ran while one was open for 0% of the time, Pallas kernels for 2%

profile of v6, /device:TPU:0, one launch (start us, length us, event | category | flops | bytes accessed | tf_op | source)
XLA Modules:
  0.0 43.2 jit_solution(17047188138681058007)
XLA Ops:
  0.0 1.3 %shard_map.28 = (bf16[64,1024]{1,0:T(8,128)(2,1)S(1)}, bf16[256,1024]{1,0:T(8,128)(2,1)S(1)}, s32[1,256]{1,0:T(1,128)S(1)}, s32[1,256]{1,0:T(1,128)S(1)}, s32[1,256]{1,0:T(1,128)S(1)}) custom-call(bf16[256,1024]{1,0:T(8,128)(2,1)} %rows_hbm.1, s32[1,256]{1,0:T(1,128)} %bitcast.2), custom_call_target="tpu_custom_call" | custom-call | flops 16777216 | bytes 1048576 | tf_op jit(solution)/shard_map/pallas_call | solution.py:22
  1.3 5.5 %collective-permute-start.13 = (bf16[64,1024]{1,0:T(8,128)(2,1)S(1)}, bf16[64,1024]{1,0:T(8,128)(2,1)S(1)}, u32[]{:S(2)}, u32[]{:S(2)}) collective-permute-start(bf16[64,1024]{1,0:T(8,128)(2,1)S(1)} %get-tuple-element.32), channel_id=1, source_target_pairs={{0,15},{1,14},{2,13},{3,12},{4,11},{5,10},{6,9},{7,8},{8,7},{9,6},... | collective-permute-start | bytes 393224 | tf_op jit(solution)/shard_map/ppermute | solution.py:191
  6.8 0.6 %shard_map.29 = (bf16[64,1024]{1,0:T(8,128)(2,1)S(1)}, bf16[64,1024]{1,0:T(8,128)(2,1)S(1)}, bf16[64,1024]{1,0:T(8,128)(2,1)S(1)}, bf16[64,1024]{1,0:T(8,128)(2,...) custom-call(bf16[256,1024]{1,0:T(8,128)(2,1)S(1)} %get-tuple-element, ...), custom_call_target="tpu_custom_call" | custom-call | flops 16777216 | bytes 1048576 | tf_op jit(solution)/shard_map/pallas_call | solution.py:22
  7.4 0.9 %collective-permute-start.1 = (bf16[64,1024]{1,0:T(8,128)(2,1)S(1)}, bf16[64,1024]{1,0:T(8,128)(2,1)S(1)}, u32[]{:S(2)}, u32[]{:S(2)}) collective-permute-start(bf16[64,1024]{1,0:T(8,128)(2,1)S(1)} %get-tuple-element.25), channel_id=1, source_target_pairs={{0,3},{1,2},{2,1},{3,0},{4,7},{5,6},{6,5},{7,4},{8,11},{9,10},{10,... | collective-permute-start | bytes 393224 | tf_op jit(solution)/shard_map/ppermute | solution.py:191
  8.3 0.0 collective-permute-start.3
  8.3 2.7 %collective-permute-start.5 = (bf16[64,1024]{1,0:T(8,128)(2,1)S(1)}, bf16[64,1024]{1,0:T(8,128)(2,1)S(1)}, u32[]{:S(2)}, u32[]{:S(2)}) collective-permute-start(bf16[64,1024]{1,0:T(8,128)(2,1)S(1)} %get-tuple-element.27), channel_id=1, source_target_pairs={{0,7},{1,6},{2,5},{3,4},{4,3},{5,2},{6,1},{7,0},{8,15},{9,14},{10,... | collective-permute-start | bytes 393224 | tf_op jit(solution)/shard_map/ppermute | solution.py:191
  11.0 0.0 collective-permute-start.7
  11.0 0.0 collective-permute-done.13.refs_0_
  11.0 4.7 %collective-permute-start.9 = (bf16[64,1024]{1,0:T(8,128)(2,1)S(1)}, bf16[64,1024]{1,0:T(8,128)(2,1)S(1)}, u32[]{:S(2)}, u32[]{:S(2)}) collective-permute-start(bf16[64,1024]{1,0:T(8,128)(2,1)S(1)} %get-tuple-element.29), channel_id=1, source_target_pairs={{0,11},{1,10},{2,9},{3,8},{4,15},{5,14},{6,13},{7,12},{8,3},{9,2},... | collective-permute-start | bytes 393224 | tf_op jit(solution)/shard_map/ppermute | solution.py:191
  15.7 0.0 collective-permute-done.1.refs_3_
  15.7 0.6 %collective-permute-start = (bf16[32,1024]{1,0:T(8,128)(2,1)S(1)}, bf16[32,1024]{1,0:T(8,128)(2,1)S(1)}, u32[]{:S(2)}, u32[]{:S(2)}) collective-permute-start(bf16[32,1024]{1,0:T(8,128)(2,1)S(1)} %get-tuple-element.24), channel_id=1, source_target_pairs={{0,1},{1,0},{2,3},{3,2},{4,5},{5,4},{6,7},{7,6},{8,9},{9,8},{10,11... | collective-permute-start | bytes 196616 | tf_op jit(solution)/shard_map/ppermute | solution.py:191
  16.3 0.0 collective-permute-done.3.refs_5_
  16.3 1.1 %collective-permute-start.11 = (bf16[32,1024]{1,0:T(8,128)(2,1)S(1)}, bf16[32,1024]{1,0:T(8,128)(2,1)S(1)}, u32[]{:S(2)}, u32[]{:S(2)}) collective-permute-start(bf16[32,1024]{1,0:T(8,128)(2,1)S(1)} %get-tuple-element.30), channel_id=1, source_target_pairs={{0,12},{1,13},{2,14},{3,15},{4,8},{5,9},{6,10},{7,11},{8,4},{9,5},... | collective-permute-start | bytes 196616 | tf_op jit(solution)/shard_map/ppermute | solution.py:191
  17.4 2.8 %collective-permute-done.5.refs_7_ = bf16[64,1024]{1,0:T(8,128)(2,1)S(1)} collective-permute-done((bf16[64,1024]{1,0:T(8,128)(2,1)S(1)}, bf16[64,1024]{1,0:T(8,128)(2,1)S(1)}, u32[]{:S(2)}, u32[]{:S(2)}) %collective-permute-start.5) | collective-permute-done | bytes 131104 | tf_op jit(solution)/shard_map/ppermute | solution.py:191
  20.2 3.8 %collective-permute-start.12 = (bf16[32,1024]{1,0:T(8,128)(2,1)S(1)}, bf16[32,1024]{1,0:T(8,128)(2,1)S(1)}, u32[]{:S(2)}, u32[]{:S(2)}) collective-permute-start(bf16[32,1024]{1,0:T(8,128)(2,1)S(1)} %get-tuple-element.31), channel_id=1, source_target_pairs={{0,13},{1,12},{2,15},{3,14},{4,9},{5,8},{6,11},{7,10},{8,5},{9,4},... | collective-permute-start | bytes 196616 | tf_op jit(solution)/shard_map/ppermute | solution.py:191
  24.0 0.7 %collective-permute-done.7.refs_9_ = bf16[64,1024]{1,0:T(8,128)(2,1)S(1)} collective-permute-done((bf16[64,1024]{1,0:T(8,128)(2,1)S(1)}, bf16[64,1024]{1,0:T(8,128)(2,1)S(1)}, u32[]{:S(2)}, u32[]{:S(2)}) %collective-permute-start.7) | collective-permute-done | bytes 131104 | tf_op jit(solution)/shard_map/ppermute | solution.py:191
  24.7 0.2 collective-permute-start.14
  24.9 3.9 %collective-permute-done.9.refs_11_ = bf16[64,1024]{1,0:T(8,128)(2,1)S(1)} collective-permute-done((bf16[64,1024]{1,0:T(8,128)(2,1)S(1)}, bf16[64,1024]{1,0:T(8,128)(2,1)S(1)}, u32[]{:S(2)}, u32[]{:S(2)}) %collective-permute-start.9) | collective-permute-done | bytes 131104 | tf_op jit(solution)/shard_map/ppermute | solution.py:191
  28.8 0.1 collective-permute-start.2
  28.9 0.0 collective-permute-done.refs_1_
  28.9 0.5 %collective-permute-start.4 = (bf16[32,1024]{1,0:T(8,128)(2,1)S(1)}, bf16[32,1024]{1,0:T(8,128)(2,1)S(1)}, u32[]{:S(2)}, u32[]{:S(2)}) collective-permute-start(bf16[32,1024]{1,0:T(8,128)(2,1)S(1)} %slice.25), channel_id=1, source_target_pairs={{0,1},{1,0},{2,3},{3,2},{4,5},{5,4},{6,7},{7,6},{8,9},{9,8},{10,11... | collective-permute-start | bytes 196616 | tf_op jit(solution)/shard_map/ppermute | solution.py:191
  29.4 0.0 collective-permute-done.11.refs_12_
  29.4 0.1 collective-permute-start.6
  29.5 0.0 collective-permute-done.12.refs_13_
  29.5 0.4 collective-permute-start.8
  29.9 0.0 collective-permute-done.14.refs_1_
  29.9 0.1 collective-permute-start.10
  30.0 0.1 shard_map.30
  30.1 0.0 collective-permute-done.2.refs_2_
  30.2 0.1 collective-permute-done.4.refs_4_
  30.3 0.4 collective-permute-done.6.refs_6_
  30.6 0.2 collective-permute-done.8.refs_8_
  30.8 0.4 collective-permute-done.10.refs_10_
  31.2 0.6 %shard_map.31 = f32[16,1,128]{2,1,0:T(1,128)S(1)} custom-call(bf16[32,1024]{1,0:T(8,128)(2,1)S(1)} %get-tuple-element.23.refs_0_, bf16[32,1024]{1,0:T(8,128)(2,1)S(1)} %collective-permute-done.refs_1_, bf16[32,1024]{1,0:T(8,128)(2,1)S(1)} %collective-permute-done.2.refs_2_, bf16[64,1024]{1,0:T(8,128)(2,1)S(1)} %collective-permute-done.1.refs_3_, ...), custom_call_target="tpu_custom_call" | custom-call | flops 16777216 | bytes 1048576 | tf_op jit(solution)/shard_map/pallas_call | solution.py:22
  31.7 10.8 %all_to_all.5.best_ref = f32[16,1,128]{2,1,0:T(1,128)S(1)} all-to-all(f32[16,1,128]{2,1,0:T(1,128)S(1)} %shard_map.31), channel_id=1, replica_groups=mesh['lang'=2,'clu'=16] {'clu'}, dimensions={0} | all-to-all | bytes 16384 | tf_op jit(solution)/shard_map/all_to_all | solution.py:284
  42.5 0.7 %shard_map.32 = f32[1,256]{1,0:T(1,128)} custom-call(f32[16,1,128]{2,1,0:T(1,128)S(1)} %all_to_all.5.best_ref, s32[1,256]{1,0:T(1,128)S(1)} %get-tuple-element.35.rank_ref, s32[1,256]{1,0:T(1,128)S(1)} %get-tuple-element.36.cluster_ref), custom_call_target="tpu_custom_call" | custom-call | flops 16777216 | bytes 1048576 | tf_op jit(solution)/shard_map/pallas_call | solution.py:22
  (6 shorter events, 0.0 us)
Async XLA Ops:
  1.3 9.6 %collective-permute-start.13 = (bf16[64,1024]{1,0:T(8,128)(2,1)S(1)}, bf16[64,1024]{1,0:T(8,128)(2,1)S(1)}, u32[]{:S(2)}, u32[]{:S(2)}) collective-permute-start(bf16[64,1024]{1,0:T(8,128)(2,1)S(1)} %get-tuple-element.32), channel_id=1, source_target_pairs={{0,15},{1,14},{2,13},{3,12},{4,11},{5,10},{6,9},{7,8},{8,7},{9,6},... | collective-permute-start | bytes 393224 | tf_op jit(solution)/shard_map/ppermute | solution.py:191
  7.4 8.3 %collective-permute-start.1 = (bf16[64,1024]{1,0:T(8,128)(2,1)S(1)}, bf16[64,1024]{1,0:T(8,128)(2,1)S(1)}, u32[]{:S(2)}, u32[]{:S(2)}) collective-permute-start(bf16[64,1024]{1,0:T(8,128)(2,1)S(1)} %get-tuple-element.25), channel_id=1, source_target_pairs={{0,3},{1,2},{2,1},{3,0},{4,7},{5,6},{6,5},{7,4},{8,11},{9,10},{10,... | collective-permute-start | bytes 393224 | tf_op jit(solution)/shard_map/ppermute | solution.py:191
  8.3 8.0 %collective-permute-start.3 = (bf16[64,1024]{1,0:T(8,128)(2,1)S(1)}, bf16[64,1024]{1,0:T(8,128)(2,1)S(1)}, u32[]{:S(2)}, u32[]{:S(2)}) collective-permute-start(bf16[64,1024]{1,0:T(8,128)(2,1)S(1)} %get-tuple-element.26), channel_id=1, source_target_pairs={{0,5},{1,4},{2,7},{3,6},{4,1},{5,0},{6,3},{7,2},{8,13},{9,12},{10,... | collective-permute-start | bytes 393224 | tf_op jit(solution)/shard_map/ppermute | solution.py:191
  8.3 11.9 %collective-permute-start.5 = (bf16[64,1024]{1,0:T(8,128)(2,1)S(1)}, bf16[64,1024]{1,0:T(8,128)(2,1)S(1)}, u32[]{:S(2)}, u32[]{:S(2)}) collective-permute-start(bf16[64,1024]{1,0:T(8,128)(2,1)S(1)} %get-tuple-element.27), channel_id=1, source_target_pairs={{0,7},{1,6},{2,5},{3,4},{4,3},{5,2},{6,1},{7,0},{8,15},{9,14},{10,... | collective-permute-start | bytes 393224 | tf_op jit(solution)/shard_map/ppermute | solution.py:191
  11.0 13.7 %collective-permute-start.7 = (bf16[64,1024]{1,0:T(8,128)(2,1)S(1)}, bf16[64,1024]{1,0:T(8,128)(2,1)S(1)}, u32[]{:S(2)}, u32[]{:S(2)}) collective-permute-start(bf16[64,1024]{1,0:T(8,128)(2,1)S(1)} %get-tuple-element.28), channel_id=1, source_target_pairs={{0,9},{1,8},{2,11},{3,10},{4,13},{5,12},{6,15},{7,14},{8,1},{9,0},... | collective-permute-start | bytes 393224 | tf_op jit(solution)/shard_map/ppermute | solution.py:191
  11.0 17.8 %collective-permute-start.9 = (bf16[64,1024]{1,0:T(8,128)(2,1)S(1)}, bf16[64,1024]{1,0:T(8,128)(2,1)S(1)}, u32[]{:S(2)}, u32[]{:S(2)}) collective-permute-start(bf16[64,1024]{1,0:T(8,128)(2,1)S(1)} %get-tuple-element.29), channel_id=1, source_target_pairs={{0,11},{1,10},{2,9},{3,8},{4,15},{5,14},{6,13},{7,12},{8,3},{9,2},... | collective-permute-start | bytes 393224 | tf_op jit(solution)/shard_map/ppermute | solution.py:191
  15.7 13.2 %collective-permute-start = (bf16[32,1024]{1,0:T(8,128)(2,1)S(1)}, bf16[32,1024]{1,0:T(8,128)(2,1)S(1)}, u32[]{:S(2)}, u32[]{:S(2)}) collective-permute-start(bf16[32,1024]{1,0:T(8,128)(2,1)S(1)} %get-tuple-element.24), channel_id=1, source_target_pairs={{0,1},{1,0},{2,3},{3,2},{4,5},{5,4},{6,7},{7,6},{8,9},{9,8},{10,11... | collective-permute-start | bytes 196616 | tf_op jit(solution)/shard_map/ppermute | solution.py:191
  16.3 13.1 %collective-permute-start.11 = (bf16[32,1024]{1,0:T(8,128)(2,1)S(1)}, bf16[32,1024]{1,0:T(8,128)(2,1)S(1)}, u32[]{:S(2)}, u32[]{:S(2)}) collective-permute-start(bf16[32,1024]{1,0:T(8,128)(2,1)S(1)} %get-tuple-element.30), channel_id=1, source_target_pairs={{0,12},{1,13},{2,14},{3,15},{4,8},{5,9},{6,10},{7,11},{8,4},{9,5},... | collective-permute-start | bytes 196616 | tf_op jit(solution)/shard_map/ppermute | solution.py:191
  20.2 9.3 %collective-permute-start.12 = (bf16[32,1024]{1,0:T(8,128)(2,1)S(1)}, bf16[32,1024]{1,0:T(8,128)(2,1)S(1)}, u32[]{:S(2)}, u32[]{:S(2)}) collective-permute-start(bf16[32,1024]{1,0:T(8,128)(2,1)S(1)} %get-tuple-element.31), channel_id=1, source_target_pairs={{0,13},{1,12},{2,15},{3,14},{4,9},{5,8},{6,11},{7,10},{8,5},{9,4},... | collective-permute-start | bytes 196616 | tf_op jit(solution)/shard_map/ppermute | solution.py:191
  24.7 5.2 %collective-permute-start.14 = (bf16[32,1024]{1,0:T(8,128)(2,1)S(1)}, bf16[32,1024]{1,0:T(8,128)(2,1)S(1)}, u32[]{:S(2)}, u32[]{:S(2)}) collective-permute-start(bf16[32,1024]{1,0:T(8,128)(2,1)S(1)} %slice.29), channel_id=1, source_target_pairs={{0,1},{1,0},{2,3},{3,2},{4,5},{5,4},{6,7},{7,6},{8,9},{9,8},{10,11... | collective-permute-start | bytes 196616 | tf_op jit(solution)/shard_map/ppermute | solution.py:191
  28.8 1.4 %collective-permute-start.2 = (bf16[32,1024]{1,0:T(8,128)(2,1)S(1)}, bf16[32,1024]{1,0:T(8,128)(2,1)S(1)}, u32[]{:S(2)}, u32[]{:S(2)}) collective-permute-start(bf16[32,1024]{1,0:T(8,128)(2,1)S(1)} %slice.24), channel_id=1, source_target_pairs={{0,1},{1,0},{2,3},{3,2},{4,5},{5,4},{6,7},{7,6},{8,9},{9,8},{10,11... | collective-permute-start | bytes 196616 | tf_op jit(solution)/shard_map/ppermute | solution.py:191
  28.9 1.4 %collective-permute-start.4 = (bf16[32,1024]{1,0:T(8,128)(2,1)S(1)}, bf16[32,1024]{1,0:T(8,128)(2,1)S(1)}, u32[]{:S(2)}, u32[]{:S(2)}) collective-permute-start(bf16[32,1024]{1,0:T(8,128)(2,1)S(1)} %slice.25), channel_id=1, source_target_pairs={{0,1},{1,0},{2,3},{3,2},{4,5},{5,4},{6,7},{7,6},{8,9},{9,8},{10,11... | collective-permute-start | bytes 196616 | tf_op jit(solution)/shard_map/ppermute | solution.py:191
  29.4 1.3 %collective-permute-start.6 = (bf16[32,1024]{1,0:T(8,128)(2,1)S(1)}, bf16[32,1024]{1,0:T(8,128)(2,1)S(1)}, u32[]{:S(2)}, u32[]{:S(2)}) collective-permute-start(bf16[32,1024]{1,0:T(8,128)(2,1)S(1)} %slice.26), channel_id=1, source_target_pairs={{0,1},{1,0},{2,3},{3,2},{4,5},{5,4},{6,7},{7,6},{8,9},{9,8},{10,11... | collective-permute-start | bytes 196616 | tf_op jit(solution)/shard_map/ppermute | solution.py:191
  29.5 1.3 %collective-permute-start.8 = (bf16[32,1024]{1,0:T(8,128)(2,1)S(1)}, bf16[32,1024]{1,0:T(8,128)(2,1)S(1)}, u32[]{:S(2)}, u32[]{:S(2)}) collective-permute-start(bf16[32,1024]{1,0:T(8,128)(2,1)S(1)} %slice.27), channel_id=1, source_target_pairs={{0,1},{1,0},{2,3},{3,2},{4,5},{5,4},{6,7},{7,6},{8,9},{9,8},{10,11... | collective-permute-start | bytes 196616 | tf_op jit(solution)/shard_map/ppermute | solution.py:191
  29.9 1.3 %collective-permute-start.10 = (bf16[32,1024]{1,0:T(8,128)(2,1)S(1)}, bf16[32,1024]{1,0:T(8,128)(2,1)S(1)}, u32[]{:S(2)}, u32[]{:S(2)}) collective-permute-start(bf16[32,1024]{1,0:T(8,128)(2,1)S(1)} %slice.28), channel_id=1, source_target_pairs={{0,1},{1,0},{2,3},{3,2},{4,5},{5,4},{6,7},{7,6},{8,9},{9,8},{10,11... | collective-permute-start | bytes 196616 | tf_op jit(solution)/shard_map/ppermute | solution.py:191
